TPU v7x, 128 devices: a whole 4x4x4 slice. The times are simulated.
128 devices in a mesh: dp: 1, ep: 128 (over z, y, x, core).
Axes of the slice: x: 4, y: 4, z: 4, core: 2. Of those that a mesh axis runs over, the one named last changes fastest.
Arguments:
- tok_x: bfloat16 [16384, 2048], P(('dp', 'ep'))
- expert_ids: int32 [16384, 8], P(('dp', 'ep'))
- gates: float32 [16384, 8], P(('dp', 'ep'))
- hot_tok: int32 [8192], P(('dp', 'ep'))
- hot_gates: float32 [8192], P(('dp', 'ep'))
- w_gate: bfloat16 [128, 2048, 768], P('ep')
- w_up: bfloat16 [128, 2048, 768], P('ep')
- w_down: bfloat16 [128, 768, 2048], P('ep')
Outputs:
- output: bfloat16 [16384, 2048], P(('dp', 'ep'))
All inputs are finite; a program needn't handle non-finite values.
Results may differ from a plain program's by a relative error of at most 0.00787365.
Values are sent between devices in bfloat16 or wider.
A program may use at most 1 GiB of HBM per device.

v0:
```python
import jax
import jax.numpy as jnp
from jax import lax
from jax.sharding import PartitionSpec as P


def route_plan(flat_ids, num_experts, cold_cap):
    routes = flat_ids.shape[0]
    sort_order = jnp.argsort(flat_ids, stable=True)
    exp_counts = jnp.bincount(flat_ids, length=num_experts).astype(jnp.int32)
    exp_starts = jnp.cumsum(exp_counts) - exp_counts
    slot_pos = jnp.arange(cold_cap, dtype=jnp.int32)
    filled = slot_pos[None, :] < exp_counts[:, None]
    sorted_pos = jnp.minimum(exp_starts[:, None] + slot_pos[None, :], routes - 1)
    src_route = sort_order[sorted_pos]
    route_rank = jnp.zeros((routes,), jnp.int32).at[sort_order].set(jnp.arange(routes, dtype=jnp.int32))
    route_slot = flat_ids * cold_cap + route_rank - exp_starts[flat_ids]
    return src_route, filled, route_slot


def swiglu_rows(in_rows, w_gate_e, w_up_e, w_down_e):
    gate_act = jnp.einsum('...d,df->...f', in_rows, w_gate_e, preferred_element_type=jnp.float32)
    up_act = jnp.einsum('...d,df->...f', in_rows, w_up_e, preferred_element_type=jnp.float32)
    hidden = (jax.nn.silu(gate_act) * up_act).astype(jnp.bfloat16)
    return jnp.einsum('...f,fd->...d', hidden, w_down_e, preferred_element_type=jnp.float32).astype(jnp.bfloat16)


def combine_rows(out_rows, route_slot, gates_loc, hot_loc, hot_g_loc):
    num_tokens, top_k = gates_loc.shape
    hot_count = hot_loc.shape[0]
    cold_total = out_rows.shape[0] - hot_count
    hot_index = jnp.zeros((num_tokens,), jnp.int32).at[hot_loc].set(jnp.arange(hot_count, dtype=jnp.int32))
    hot_weight = jnp.zeros((num_tokens,), jnp.float32).at[hot_loc].set(hot_g_loc)
    all_slots = jnp.concatenate([route_slot.reshape(num_tokens, top_k), (cold_total + hot_index)[:, None]], axis=1)
    all_gates = jnp.concatenate([gates_loc, hot_weight[:, None]], axis=1)
    picked = out_rows[all_slots]
    return jnp.einsum('tk,tkd->td', all_gates, picked, preferred_element_type=jnp.float32).astype(jnp.bfloat16)


def solution(mesh):
    group_size = mesh.shape['ep']
    row_spec = P(('dp', 'ep'), None)
    list_spec = P(('dp', 'ep'))
    expert_spec = P('ep', None, None)

    def local_layer(x_loc, ids_loc, gates_loc, hot_loc, hot_g_loc, wg_loc, wu_loc, wd_loc):
        local_experts = wg_loc.shape[0]
        d_model = x_loc.shape[1]
        num_experts = local_experts * group_size
        num_tokens, top_k = ids_loc.shape
        cold_cap = (num_tokens * top_k + num_experts - 2) // (num_experts - 1)
        block_rows = local_experts * cold_cap
        src_route, filled, route_slot = route_plan(ids_loc.reshape(num_tokens * top_k), num_experts, cold_cap)
        cold_buf = jnp.where(filled[:, :, None], x_loc[src_route // top_k], 0)
        hot_buf = x_loc[hot_loc]
        to_owner = jnp.where(jnp.arange(group_size)[:, None, None] == 0, hot_buf[None], 0)
        send_buf = jnp.concatenate([cold_buf.reshape(group_size, block_rows, d_model), to_owner], axis=1)
        recv_buf = lax.all_to_all(send_buf, 'ep', 0, 0, tiled=True)
        cold_in = recv_buf[:, :block_rows].reshape(group_size, local_experts, cold_cap, d_model)
        gate_act = jnp.einsum('slcd,ldf->slcf', cold_in, wg_loc, preferred_element_type=jnp.float32)
        up_act = jnp.einsum('slcd,ldf->slcf', cold_in, wu_loc, preferred_element_type=jnp.float32)
        hidden = (jax.nn.silu(gate_act) * up_act).astype(jnp.bfloat16)
        cold_out = jnp.einsum('slcf,lfd->slcd', hidden, wd_loc, preferred_element_type=jnp.float32).astype(jnp.bfloat16)
        hot_out = lax.cond(lax.axis_index('ep') == 0,
                           lambda hot_in: swiglu_rows(hot_in, wg_loc[0], wu_loc[0], wd_loc[0]),
                           jnp.zeros_like, recv_buf[:, block_rows:])
        back_buf = jnp.concatenate([cold_out.reshape(group_size, block_rows, d_model), hot_out], axis=1)
        ret_buf = lax.all_to_all(back_buf, 'ep', 0, 0, tiled=True)
        out_rows = jnp.concatenate([ret_buf[:, :block_rows].reshape(num_experts * cold_cap, d_model),
                                    ret_buf[0, block_rows:]], axis=0)
        return combine_rows(out_rows, route_slot, gates_loc, hot_loc, hot_g_loc)

    return jax.shard_map(local_layer, mesh=mesh,
                         in_specs=(row_spec, row_spec, row_spec, list_spec, list_spec, expert_spec, expert_spec, expert_spec),
                         out_specs=row_spec, check_vma=False)
```

profile of v0, /device:TPU:2, one launch (start us, length us, event | category | flops | bytes accessed | tf_op | source)
XLA Modules:
  0.0 1756.6 jit_solution(11614078775448314433)
XLA Ops:
  0.0 0.8 copy.31
  1.0 0.1 reshape.308
  1.1 0.7 compare_select_fusion.5
  1.7 0.5 copy-done.11
  2.2 0.6 compare_select_fusion.3
  2.8 7.6 scatter_custom_fusion.1
  10.5 0.1 copy.33
  10.6 0.2 reduce-window.9
  10.8 0.1 reduce
  10.9 0.5 copy-done.4
  11.5 0.2 reshape.319
  11.8 4.4 sort.17
  16.1 4.6 gather_fusion
  20.7 0.2 gather.18
  21.0 0.2 reshape.327
  21.2 0.7 gather_fusion.2
  22.0 5.9 gather_fusion.1
  27.9 8.0 reshape.326
  35.9 10.9 broadcast_select_fusion
  46.9 7.3 broadcast_select_fusion.1
  54.1 28.6 %pad_maximum_fusion = bf16[128,73,2048]{2,1,0:T(8,128)(2,1)} fusion(bf16[128,64,2048]{2,1,0:T(8,128)(2,1)} %broadcast_select_fusion, bf16[128,9,2048]{2,1,0:T(8,128)(2,1)} %broadcast_select_fusion.1), kind=kLoop, calls=%fused_computation.20 | loop fusion | flops 76546048 | bytes 76546048 | tf_op jit(solution)/shard_map/concatenate | solution.py:57
  82.7 11.6 all-to-all-start
  94.4 711.2 %all-to-all-done = bf16[128,73,2048]{2,1,0:T(8,128)(2,1)} async-done(((bf16[128,73,2048]{2,1,0:T(8,128)(2,1)}), bf16[128,73,2048]{2,1,0:T(8,128)(2,1)}, u32[]{:S(2)}, u32[]{:S(2)}) %all-to-all-start) | async-done | bytes 38273056 | tf_op jit(solution)/shard_map/all_to_all | solution.py:58
  805.6 8.4 slice.27
  814.0 13.3 fusion.19
  827.4 9.7 fusion.14
  837.1 4.3 convolution_convert_fusion.1
  841.3 6.4 copy.36
  847.8 18.6 %conditional.1 = (bf16[128,64,2048]{2,1,0:T(8,128)(2,1)}) conditional(s32[]{:T(128)} %convert_element_type.27, () %tuple.11, (bf16[1,2048,768]{2,1,0:T(8,128)(2,1)S(1)}, bf16[128,73,2048]{2,1,0:T(8,128)(2,1)}, bf16[1,2048,768]{2,1,0:T(8,128)(2,1)S(1)}, bf16[1,768,2048]{2,1,0:T(8,128)(2,1)}) %tuple.21), branch_computations={%region_4.5_spmd, %region_5.6_spmd} | conditional | flops 77363937280 | bytes 274726944 | solution.py:64
  847.8 11.0 broadcast.182.clone
  866.4 28.6 %pad_maximum_fusion.1 = bf16[128,73,2048]{2,1,0:T(8,128)(2,1)} fusion(bf16[128,64,2048]{2,1,0:T(8,128)(2,1)} %get-tuple-element.31, bf16[128,9,2048]{2,1,0:T(8,128)(2,1)} %copy.36), kind=kLoop, calls=%fused_computation.21 | loop fusion | flops 76546048 | bytes 76546048 | tf_op jit(solution)/shard_map/concatenate | solution.py:67
  895.0 123.2 %all-to-all-start.1 = ((bf16[128,73,2048]{2,1,0:T(8,128)(2,1)}), bf16[128,73,2048]{2,1,0:T(8,128)(2,1)}, u32[]{:S(2)}, u32[]{:S(2)}) async-start(bf16[128,73,2048]{2,1,0:T(8,128)(2,1)} %pad_maximum_fusion.1), calls=%async_computation.1 | async-start | bytes 83886080 | tf_op jit(solution)/shard_map/all_to_all | solution.py:68
  1018.2 0.9 scatter_custom_fusion
  1019.2 0.1 copy.39
  1019.3 0.9 scatter_custom_fusion.3
  1020.2 0.1 copy.38
  1020.4 6.6 gather_fusion.3
  1027.0 4.3 scatter_custom_fusion.2
  1031.5 0.2 reshape.351
  1031.7 673.8 %all-to-all-done.1 = bf16[128,73,2048]{2,1,0:T(8,128)(2,1)} async-done(((bf16[128,73,2048]{2,1,0:T(8,128)(2,1)}), bf16[128,73,2048]{2,1,0:T(8,128)(2,1)}, u32[]{:S(2)}, u32[]{:S(2)}) %all-to-all-start.1) | async-done | bytes 38273056 | tf_op jit(solution)/shard_map/all_to_all | solution.py:68
  1705.6 8.3 slice.28
  1713.8 8.5 reshape.316
  1722.3 1.0 slice_bitcast_fusion
  1723.3 5.3 pad_maximum_fusion.2
  1728.7 13.7 gather_fusion.4
  1742.4 8.1 reshape.350
  1750.5 4.8 fusion.38
  1755.3 1.1 copy.60
  (49 shorter events, 0.6 us)
Async XLA Ops:
  0.0 21.2 %copy-start = (bf16[128,2048]{1,0:T(8,128)(2,1)S(1)}, bf16[128,2048]{1,0:T(8,128)(2,1)}, u32[]{:S(2)}) copy-start(bf16[128,2048]{1,0:T(8,128)(2,1)} %param.10) | copy-start | bytes 1572868
  0.9 19.8 %copy-start.7 = (s32[1024]{0:T(1024)}, s32[1024]{0:T(1024)S(1)}, u32[]{:S(2)}) copy-start(s32[1024]{0:T(1024)S(1)} %reshape.309) | copy-start | bytes 12292
  1.7 0.5 copy-start.11
  10.9 0.5 copy-start.4
  16.1 4.6 copy-start.2
  82.7 722.9 %all-to-all-start = ((bf16[128,73,2048]{2,1,0:T(8,128)(2,1)}), bf16[128,73,2048]{2,1,0:T(8,128)(2,1)}, u32[]{:S(2)}, u32[]{:S(2)}) async-start(bf16[128,73,2048]{2,1,0:T(8,128)(2,1)} %pad_maximum_fusion), calls=%async_computation | async-start | bytes 83886080 | tf_op jit(solution)/shard_map/all_to_all | solution.py:58
  805.6 8.4 copy-start.13
  814.0 13.3 copy-start.6
  814.0 13.3 copy-start.12
  827.4 9.7 copy-start.15
  895.0 124.2 %copy-start.10 = (f32[128,8]{0,1:T(8,128)S(1)}, f32[128,8]{0,1:T(8,128)}, u32[]{:S(2)}) copy-start(f32[128,8]{0,1:T(8,128)} %param.12) | copy-start | bytes 12292
  895.0 125.4 %copy-start.9 = (s32[1024,1]{0,1:T(1,128)S(1)}, s32[1024,1]{0,1:T(1,128)}, u32[]{:S(2)}) copy-start(s32[1024,1]{0,1:T(1,128)} %get-tuple-element.32) | copy-start | bytes 12292
  895.0 125.4 %copy-start.5 = (s32[128]{0:T(128)S(1)}, s32[128]{0:T(128)}, u32[]{:S(2)}) copy-start(s32[128]{0:T(128)} %copy-done.4) | copy-start | bytes 1540
  895.0 131.9 %copy-start.3 = (s32[1024]{0:T(1024)S(1)}, s32[1024]{0:T(1024)}, u32[]{:S(2)}) copy-start(s32[1024]{0:T(1024)} %copy-done.2) | copy-start | bytes 12292
  895.0 136.3 %copy-start.8 = (s32[1024]{0:T(1024)S(1)}, s32[1024]{0:T(1024)}, u32[]{:S(2)}) copy-start(s32[1024]{0:T(1024)} %copy-done.7) | copy-start | bytes 12292
  895.0 810.5 %all-to-all-start.1 = ((bf16[128,73,2048]{2,1,0:T(8,128)(2,1)}), bf16[128,73,2048]{2,1,0:T(8,128)(2,1)}, u32[]{:S(2)}, u32[]{:S(2)}) async-start(bf16[128,73,2048]{2,1,0:T(8,128)(2,1)} %pad_maximum_fusion.1), calls=%async_computation.1 | async-start | bytes 83886080 | tf_op jit(solution)/shard_map/all_to_all | solution.py:68
  1742.4 14.0 copy-start.1
where the time goes:
time: 1780 us; the launch traced here: 1760 us
  waiting for transfers between devices  1390 us (78%)
  starting transfers between devices  135 us (8%)
  local copies, waits for them, and re-layouts  102 us (6%)
  other arithmetic  94.6 us (5%)
  matrix products  32 us (2%)
    all_to_all x1, waiting for transfers between devices, local_layer(): recv_buf = lax.all_to_all(send_buf, 'ep', 0, 0, tiled=True)  711 us
    all_to_all x1, waiting for transfers between devices, local_layer(): ret_buf = lax.all_to_all(back_buf, 'ep', 0, 0, tiled=True)  674 us
    all_to_all x1, starting transfers between devices, local_layer(): ret_buf = lax.all_to_all(back_buf, 'ep', 0, 0, tiled=True)  123 us
  transfers between devices with their start and end apart: 2, of which 2 were waited for; matrix products, arithmetic and copies ran while one was open for 1% of the time, Pallas kernels for 0%

commit v1 on v0

v1 whole, which is shorter than its diff:
```python
import functools

import jax
import jax.numpy as jnp
from jax import lax
from jax.experimental import pallas as pl
from jax.experimental.pallas import tpu as pltpu
from jax.sharding import PartitionSpec as P

F32 = jnp.float32
BF16 = jnp.bfloat16
SLOTS = 8
FOLD = 8
VMEM_LIMIT = 60 * 1024 * 1024


def dotf(a, b):
    return jnp.dot(a, b, preferred_element_type=F32)


def iota(shape, dim):
    return lax.broadcasted_iota(jnp.int32, shape, dim)


def dispatch_kernel(ids_ref, x_ref, out_ref):
    top_k, tokens = ids_ref.shape
    d_model = x_ref.shape[1]
    rows = out_ref.shape[0]
    piece = d_model // FOLD
    row = iota((rows, tokens), 0)
    expert = row // SLOTS
    member = jnp.zeros((rows, tokens), jnp.bool_)
    for j in range(top_k):
        member = jnp.logical_or(member, ids_ref[j:j + 1, :] == expert)
    member_f = jnp.where(member, 1.0, 0.0)
    earlier = jnp.where(iota((tokens, tokens), 0) < iota((tokens, tokens), 1), 1.0, 0.0).astype(BF16)
    rank = dotf(member_f.astype(BF16), earlier)
    slot = (row % SLOTS).astype(F32)
    pick = jnp.where(rank == slot, member_f, 0.0).astype(BF16)
    ninth = jnp.where(rank == float(SLOTS), member_f, 0.0)
    for c in range(0, d_model, 512):
        out_ref[:, c:c + 512] = dotf(pick, x_ref[:, c:c + 512]).astype(BF16)
    total = jnp.zeros((rows, piece), F32)
    for f in range(FOLD):
        pick_f = jnp.where(slot == float(f), ninth, 0.0).astype(BF16)
        total += dotf(pick_f, x_ref[:, f * piece:(f + 1) * piece])
    out_ref[:, d_model:] = total.astype(BF16)


def expert_kernel(in_ref, wg_ref, wu_ref, wd_ref, out_ref, x_ref, u_ref):
    step = pl.program_id(0)
    rows = in_ref.shape[0]
    d_model = wg_ref.shape[0]
    width = wg_ref.shape[1]
    groups = rows // SLOTS
    piece = d_model // FOLD
    all_rows = rows + groups

    @pl.when(step == 0)
    def _():
        x_ref[:rows] = in_ref[:, :d_model]
        for f in range(FOLD):
            pick = jnp.where(iota((groups, rows), 1) == iota((groups, rows), 0) * FOLD + f, 1.0, 0.0).astype(BF16)
            x_ref[rows:, f * piece:(f + 1) * piece] = dotf(pick, in_ref[:, d_model:]).astype(BF16)

    half = all_rows // 2
    for m in range(2):
        sl = slice(m * half, (m + 1) * half)
        gate = dotf(x_ref[sl], wg_ref[...])
        up = dotf(x_ref[sl], wu_ref[...])
        u_ref[sl, pl.ds(pl.multiple_of(step * width, width), width)] = (jax.nn.silu(gate) * up).astype(BF16)

    @pl.when(step == pl.num_programs(0) - 1)
    def _():
        total = jnp.zeros((rows, piece), F32)
        for f in range(FOLD):
            cols = slice(f * piece, (f + 1) * piece)
            out = dotf(u_ref[...], wd_ref[:, cols]).astype(BF16)
            out_ref[:, cols] = out[:rows]
            spread = jnp.where(iota((rows, groups), 0) == iota((rows, groups), 1) * FOLD + f, 1.0, 0.0).astype(BF16)
            total += dotf(spread, out[rows:])
        out_ref[:, d_model:] = total.astype(BF16)


def hot_kernel(x_ref, wg_ref, wu_ref, wd_ref, out_ref, acc_ref):
    step = pl.program_id(0)
    gate = dotf(x_ref[...], wg_ref[...])
    up = dotf(x_ref[...], wu_ref[...])
    part = dotf((jax.nn.silu(gate) * up).astype(BF16), wd_ref[...])

    @pl.when(step == 0)
    def _():
        acc_ref[...] = part

    @pl.when(step > 0)
    def _():
        acc_ref[...] += part

    @pl.when(step == pl.num_programs(0) - 1)
    def _():
        out_ref[...] = acc_ref[...].astype(BF16)


def three_terms(a):
    hi = a.astype(BF16)
    rest = a - hi.astype(F32)
    mid = rest.astype(BF16)
    low = (rest - mid.astype(F32)).astype(BF16)
    return jnp.concatenate([hi, mid, low], axis=0)


def combine_kernel(ids_ref, gates_ref, hot_tok_ref, hot_gate_ref, hot_ref, back_ref, y_ref):
    tokens, top_k = ids_ref.shape
    rows = back_ref.shape[0]
    d_model = y_ref.shape[1]
    piece = d_model // FOLD
    col = iota((tokens, rows), 1)
    expert = col // SLOTS
    member = jnp.zeros((tokens, rows), jnp.bool_)
    weight = jnp.zeros((tokens, rows), F32)
    for j in range(top_k):
        here = ids_ref[:, j:j + 1] == expert
        member = jnp.logical_or(member, here)
        weight = jnp.where(here, gates_ref[:, j:j + 1], weight)
    earlier = jnp.where(iota((tokens, tokens), 1) < iota((tokens, tokens), 0), 1.0, 0.0).astype(BF16)
    rank = dotf(earlier, jnp.where(member, 1.0, 0.0).astype(BF16))
    slot = (col % SLOTS).astype(F32)
    main = three_terms(jnp.where(rank == slot, weight, 0.0))
    ninth = three_terms(jnp.where(rank == float(SLOTS), weight, 0.0))
    slot3 = (iota((3 * tokens, rows), 1) % SLOTS)
    count = hot_tok_ref.shape[1]
    same = iota((tokens, count), 0) == hot_tok_ref[...]
    hot_weight = jnp.sum(jnp.where(same, hot_gate_ref[...], 0.0), axis=1, keepdims=True)
    is_hot = jnp.sum(jnp.where(same, 1.0, 0.0), axis=1, keepdims=True) > 0.5
    for f in range(FOLD):
        cols = slice(f * piece, (f + 1) * piece)
        ninth_f = jnp.where(slot3 == f, ninth, jnp.zeros_like(ninth))
        terms = dotf(main, back_ref[:, cols]) + dotf(ninth_f, back_ref[:, d_model:])
        total = terms[2 * tokens:] + terms[tokens:2 * tokens] + terms[:tokens]
        hot = jnp.where(is_hot, hot_weight * hot_ref[:, cols].astype(F32), 0.0)
        y_ref[:, cols] = (total + hot).astype(BF16)


def vmem(n):
    return [pl.BlockSpec(memory_space=pltpu.VMEM)] * n


def params(**kw):
    return pltpu.CompilerParams(vmem_limit_bytes=VMEM_LIMIT, **kw)


def solution(mesh):
    group_size = mesh.shape['ep']
    row_spec = P(('dp', 'ep'), None)
    list_spec = P(('dp', 'ep'))
    expert_spec = P('ep', None, None)

    def local_layer(x, ids, gates, hot_tok, hot_gates, wg, wu, wd):
        wg, wu, wd = wg[0], wu[0], wd[0]
        tokens, d_model = x.shape
        d_ff = wg.shape[1]
        rows = group_size * SLOTS
        width = d_model + d_model // FOLD
        split = 3
        blk = d_ff // split

        first = lax.axis_index('ep') == 0
        hot_w = [lax.psum(jnp.where(first, w, jnp.zeros_like(w)), 'ep') for w in (wg, wu, wd)]

        send = pl.pallas_call(
            dispatch_kernel, out_shape=jax.ShapeDtypeStruct((rows, width), BF16),
            in_specs=vmem(2), out_specs=vmem(1)[0], compiler_params=params(), name="dispatch",
        )(ids.T, x)
        recv = lax.all_to_all(send.reshape(group_size, SLOTS, width), 'ep', 0, 0, tiled=True)
        whole = lambda shape: pl.BlockSpec(shape, lambda i: (0, 0))
        wide = pl.BlockSpec((d_model, blk), lambda i: (0, i))
        out = pl.pallas_call(
            expert_kernel, out_shape=jax.ShapeDtypeStruct((rows, width), BF16), grid=(split,),
            in_specs=[whole((rows, width)), wide, wide, whole((d_ff, d_model))],
            out_specs=whole((rows, width)),
            scratch_shapes=[pltpu.VMEM((rows + group_size, d_model), BF16), pltpu.VMEM((rows + group_size, d_ff), BF16)],
            compiler_params=params(), name="expert",
        )(recv.reshape(rows, width), wg, wu, wd)
        back = lax.all_to_all(out.reshape(group_size, SLOTS, width), 'ep', 0, 0, tiled=True)
        hot_out = pl.pallas_call(
            hot_kernel, out_shape=jax.ShapeDtypeStruct((tokens, d_model), BF16), grid=(split,),
            in_specs=[whole((tokens, d_model)), wide, wide, pl.BlockSpec((blk, d_model), lambda i: (i, 0))],
            out_specs=whole((tokens, d_model)), scratch_shapes=[pltpu.VMEM((tokens, d_model), F32)],
            compiler_params=params(), name="hot",
            cost_estimate=pl.CostEstimate(flops=6 * tokens * d_model * d_ff, bytes_accessed=6 * d_model * d_ff, transcendentals=0),
        )(x, *hot_w)
        return pl.pallas_call(
            combine_kernel, out_shape=jax.ShapeDtypeStruct((tokens, d_model), BF16),
            in_specs=vmem(6), out_specs=vmem(1)[0], compiler_params=params(), name="combine",
        )(ids, gates, hot_tok[None, :], hot_gates[None, :], hot_out, back.reshape(rows, width))

    return jax.shard_map(local_layer, mesh=mesh,
                         in_specs=(row_spec, row_spec, row_spec, list_spec, list_spec, expert_spec, expert_spec, expert_spec),
                         out_specs=row_spec, check_vma=False)
```

time: 1780 us -> 292 us (0.16); the launches traced: 1760 us -> 291 us
  waiting for transfers between devices: 1390 us -> 210 us
  starting transfers between devices: 135 us -> 17.1 us
  local copies, waits for them, and re-layouts: 102 us -> 3.52 us
  other arithmetic: 94.6 us -> 4.91 us
  Pallas kernels: 0 us -> 42 us
  matrix products: 32 us -> 0 us
    all_to_all x2, waiting for transfers between devices: 1390 us -> 56.9 us  [the longest x1 56.9 us: local_layer(): lax.all_to_all(send.reshape(group_size, SLOTS, width), 'ep', 0, 0, tiled=...]
    psum x0 -> x1, waiting for transfers between devices: none -> 153 us  [local_layer(): lax.psum(jnp.where(first, w, jnp.zeros_like(w)), 'ep')]
    all_to_all x2, starting transfers between devices: 135 us -> 16.8 us  [the longest x1 10.9 us: local_layer(): lax.all_to_all(send.reshape(group_size, SLOTS, width), 'ep', 0, 0, tiled=...]
    concatenate x5 -> x0, other arithmetic: 62.5 us -> none  [the longest x1 28.6 us: local_layer(): jnp.concatenate([cold_out.reshape(group_size, block_rows, d_model), hot_o...]
    gather x8 -> x0, local copies, waits for them, and re-layouts: 47.9 us -> none  [the longest x2 21.9 us: combine_rows(): picked = out_rows[all_slots]]
    pallas_call x0 -> x4, Pallas kernels: none -> 42 us  [the longest x1 21.2 us: local_layer(): pl.pallas_call(expert_kernel, out_shape=jax.ShapeDtypeStruct((rows, width...]
    dot_general x4 -> x0, matrix products: 32 us -> none  [the longest x1 13.3 us: local_layer(): jnp.einsum('slcd,ldf->slcf', cold_in, wu_loc, preferred_element_type=jnp....]
  transfers between devices with their start and end apart: 2 -> 3, of which waited for: 2 -> 2; matrix products, arithmetic and copies ran while one was open for 1% -> 2% of each run, Pallas kernels for 0% -> 10%
where the time goes in v1:
time: 292 us; the launch traced here: 291 us
  waiting for transfers between devices  210 us (72%)
  Pallas kernels  42 us (14%)
  starting transfers between devices  17.1 us (6%)
  between operations  13.5 us (5%)
  other arithmetic  4.91 us (2%)
  local copies, waits for them, and re-layouts  3.52 us (1%)
    psum x1, waiting for transfers between devices, local_layer(): lax.psum(jnp.where(first, w, jnp.zeros_like(w)), 'ep')  153 us
    all_to_all x1, waiting for transfers between devices, local_layer(): lax.all_to_all(send.reshape(group_size, SLOTS, width), 'ep', 0, 0, tiled=...  56.9 us
    pallas_call x1, Pallas kernels, local_layer(): pl.pallas_call(expert_kernel, out_shape=jax.ShapeDtypeStruct((rows, width...  21.2 us
    all_to_all x1, starting transfers between devices, local_layer(): lax.all_to_all(send.reshape(group_size, SLOTS, width), 'ep', 0, 0, tiled=...  10.9 us
    pallas_call x1, Pallas kernels, local_layer(): pl.pallas_call(combine_kernel, out_shape=jax.ShapeDtypeStruct((tokens, d_...  7.9 us
    pallas_call x1, Pallas kernels, local_layer(): pl.pallas_call(hot_kernel, out_shape=jax.ShapeDtypeStruct((tokens, d_mode...  6.68 us
    pallas_call x1, Pallas kernels, local_layer(): pl.pallas_call(dispatch_kernel, out_shape=jax.ShapeDtypeStruct((rows, wid...  6.15 us
    all_to_all x1, starting transfers between devices, local_layer(): lax.all_to_all(out.reshape(group_size, SLOTS, width), 'ep', 0, 0, tiled=T...  5.91 us
  transfers between devices with their start and end apart: 3, of which 2 were waited for; matrix products, arithmetic and copies ran while one was open for 2% of the time, Pallas kernels for 10%

profile of v1, /device:TPU:2, one launch (start us, length us, event | category | flops | bytes accessed | tf_op | source)
XLA Modules:
  0.0 290.8 jit_solution(11949050903964550882)
XLA Ops:
  6.5 6.2 %dispatch.1 = bf16[1024,2304]{1,0:T(8,128)(2,1)} custom-call(s32[8,128]{1,0:T(8,128)} %bitcast.18, bf16[128,2048]{1,0:T(8,128)(2,1)} %x_ref.3), custom_call_target="tpu_custom_call" | custom-call | tf_op jit(solution)/shard_map/dispatch/pallas_call | solution.py:170
  12.7 0.0 copy-start
  12.7 10.9 %all-to-all-start = ((bf16[128,8,2304]{2,1,0:T(8,128)(2,1)}), bf16[128,8,2304]{2,1,0:T(8,128)(2,1)}, u32[]{:S(2)}, u32[]{:S(2)}) async-start(bf16[128,8,2304]{2,1,0:T(8,128)(2,1)} %bitcast.13), calls=%async_computation | async-start | bytes 9437184 | tf_op jit(solution)/shard_map/all_to_all | solution.py:174
  23.6 0.2 all-reduce.3.cloned.1.call-start
  23.9 0.0 copy-done
  23.9 0.0 copy-start.1
  23.9 0.0 copy-start.2
  23.9 1.9 broadcast_select_fusion
  25.8 1.1 copy-done.1
  26.9 1.0 copy-done.2
  27.9 3.0 %broadcast_select_fusion.1 = (bf16[2048,768]{1,0:T(8,128)(2,1)}, bf16[2048,768]{1,0:T(8,128)(2,1)}) fusion(pred[]{:T(512)S(6)} %eq.3, bf16[1,2048,768]{2,1,0:T(8,128)(2,1)S(1)} %copy-done.1, bf16[1,2048,768]{2,1,0:T(8,128)(2,1)S(1)} %copy-done.2), kind=kLoop, calls=%fused_computation.1 | loop fusion | flops 3145728 | bytes 12582913 | tf_op jit(solution)/shard_map/jit(_where)/select_n | solution.py:168
  30.9 0.0 all-reduce.3.cloned.1.call-update
  30.9 56.9 %all-to-all-done = bf16[128,8,2304]{2,1,0:T(8,128)(2,1)} async-done(((bf16[128,8,2304]{2,1,0:T(8,128)(2,1)}), bf16[128,8,2304]{2,1,0:T(8,128)(2,1)}, u32[]{:S(2)}, u32[]{:S(2)}) %all-to-all-start) | async-done | bytes 4718624 | tf_op jit(solution)/shard_map/all_to_all | solution.py:174
  87.8 21.2 %expert.1 = bf16[1024,2304]{1,0:T(8,128)(2,1)} custom-call(bf16[1024,2304]{1,0:T(8,128)(2,1)} %bitcast.7.in_ref, bf16[2048,768]{1,0:T(8,128)(2,1)} %bitcast.17, bf16[2048,768]{1,0:T(8,128)(2,1)} %bitcast.16, bf16[768,2048]{1,0:T(8,128)(2,1)} %bitcast.15), custom_call_target="tpu_custom_call" | custom-call | tf_op jit(solution)/shard_map/expert/pallas_call | solution.py:177
  109.0 0.0 copy-start.3
  109.0 0.0 copy-start.4
  109.0 5.9 %all-to-all-start.1 = ((bf16[128,8,2304]{2,1,0:T(8,128)(2,1)}), bf16[128,8,2304]{2,1,0:T(8,128)(2,1)}, u32[]{:S(2)}, u32[]{:S(2)}) async-start(bf16[128,8,2304]{2,1,0:T(8,128)(2,1)} %bitcast.14), calls=%async_computation.1 | async-start | bytes 9437184 | tf_op jit(solution)/shard_map/all_to_all | solution.py:184
  114.9 0.0 copy-done.3
  114.9 0.7 copy.9.ids_ref
  115.7 0.0 copy-done.4
  115.7 0.7 copy.10.gates_ref
  116.4 152.9 %all-reduce.3.cloned.1.call-done = (bf16[2048,768]{1,0:T(8,128)(2,1)}, bf16[2048,768]{1,0:T(8,128)(2,1)}, bf16[768,2048]{1,0:T(8,128)(2,1)}) async-done(((bf16[2048,768]{1,0:T(8,128)(2,1)}, bf16[2048,768]{1,0:T(8,128)(2,1)}, bf16[768,2048]{1,0:T(8,128)(2,1)}), (bf16[2048,768]{1,0:T(8,128)(2,1)}, bf16[2048,768]{1,0:T(8,128)(2,1)}, bf16[768,2048]{1,0:T(8,128)(2,1)})) %all-reduce.3.cloned.1.call-update) | async-done | bytes 9437200 | tf_op jit(solution)/shard_map/psum | solution.py:168
  269.3 6.7 %hot.1.hot_ref = bf16[128,2048]{1,0:T(8,128)(2,1)} custom-call(bf16[128,2048]{1,0:T(8,128)(2,1)} %x_ref.3, bf16[2048,768]{1,0:T(8,128)(2,1)} %get-tuple-element.5.wg_ref, bf16[2048,768]{1,0:T(8,128)(2,1)} %get-tuple-element.6.wu_ref, bf16[768,2048]{1,0:T(8,128)(2,1)} %get-tuple-element.7.wd_ref), custom_call_target="tpu_custom_call" | custom-call | flops 1207959552 | bytes 9437184 | tf_op jit(solution)/shard_map/hot/pallas_call | solution.py:185
  276.0 0.0 all-to-all-done.1
  276.0 7.9 %combine.1 = bf16[128,2048]{1,0:T(8,128)(2,1)} custom-call(s32[128,8]{1,0:T(8,128)} %copy.9.ids_ref, f32[128,8]{1,0:T(8,128)} %copy.10.gates_ref, s32[1,64]{1,0:T(1,128)} %bitcast.19, f32[1,64]{1,0:T(1,128)} %bitcast.20, bf16[128,2048]{1,0:T(8,128)(2,1)} %hot.1.hot_ref, bf16[1024,2304]{1,0:T(8,128)(2,1)} %bitcast.9.back_ref), custom_call_target="tpu_custom_call" | custom-call | tf_op jit(solution)/shard_map/combine/pallas_call | solution.py:192
Async XLA Ops:
  12.7 11.2 %copy-start = (bf16[1,768,2048]{2,1,0:T(8,128)(2,1)S(1)}, bf16[1,768,2048]{2,1,0:T(8,128)(2,1)}, u32[]{:S(2)}) copy-start(bf16[1,768,2048]{2,1,0:T(8,128)(2,1)} %param.15) | copy-start | bytes 9437188
  12.7 75.1 %all-to-all-start = ((bf16[128,8,2304]{2,1,0:T(8,128)(2,1)}), bf16[128,8,2304]{2,1,0:T(8,128)(2,1)}, u32[]{:S(2)}, u32[]{:S(2)}) async-start(bf16[128,8,2304]{2,1,0:T(8,128)(2,1)} %bitcast.13), calls=%async_computation | async-start | bytes 9437184 | tf_op jit(solution)/shard_map/all_to_all | solution.py:174
  23.6 245.7 %all-reduce.3.cloned.1.call-start = ((), (), s32[]{:S(2)}) async-start(), calls=%async_computation.2 | async-start | bytes 18874368 | tf_op jit(solution)/shard_map/psum | solution.py:168
  23.9 3.0 %copy-start.1 = (bf16[1,2048,768]{2,1,0:T(8,128)(2,1)S(1)}, bf16[1,2048,768]{2,1,0:T(8,128)(2,1)}, u32[]{:S(2)}) copy-start(bf16[1,2048,768]{2,1,0:T(8,128)(2,1)} %param.14) | copy-start | bytes 9437188
  23.9 4.0 %copy-start.2 = (bf16[1,2048,768]{2,1,0:T(8,128)(2,1)S(1)}, bf16[1,2048,768]{2,1,0:T(8,128)(2,1)}, u32[]{:S(2)}) copy-start(bf16[1,2048,768]{2,1,0:T(8,128)(2,1)} %param.13) | copy-start | bytes 9437188
  109.0 5.9 %copy-start.3 = (s32[128,8]{0,1:T(8,128)S(1)}, s32[128,8]{0,1:T(8,128)}, u32[]{:S(2)}) copy-start(s32[128,8]{0,1:T(8,128)} %param.9) | copy-start | bytes 12292
  109.0 6.7 %copy-start.4 = (f32[128,8]{0,1:T(8,128)S(1)}, f32[128,8]{0,1:T(8,128)}, u32[]{:S(2)}) copy-start(f32[128,8]{0,1:T(8,128)} %param.10) | copy-start | bytes 12292
  109.0 167.0 %all-to-all-start.1 = ((bf16[128,8,2304]{2,1,0:T(8,128)(2,1)}), bf16[128,8,2304]{2,1,0:T(8,128)(2,1)}, u32[]{:S(2)}, u32[]{:S(2)}) async-start(bf16[128,8,2304]{2,1,0:T(8,128)(2,1)} %bitcast.14), calls=%async_computation.1 | async-start | bytes 9437184 | tf_op jit(solution)/shard_map/all_to_all | solution.py:184
Sparse Core Ops, SparseCore 0:
  31.0 238.2 all-reduce.2

commit v2 on v0

v2 whole, which is shorter than its diff:
```python
import functools

import jax
import jax.numpy as jnp
from jax import lax
from jax.experimental import pallas as pl
from jax.experimental.pallas import tpu as pltpu
from jax.sharding import PartitionSpec as P

F32 = jnp.float32
BF16 = jnp.bfloat16
SLOTS = 8
FOLD = 8
VMEM_LIMIT = 60 * 1024 * 1024


def dotf(a, b):
    return jnp.dot(a, b, preferred_element_type=F32)


def iota(shape, dim):
    return lax.broadcasted_iota(jnp.int32, shape, dim)


def ones_where(mask):
    return jnp.where(mask, 1.0, 0.0).astype(BF16)


def three_terms(a):
    hi = a.astype(BF16)
    rest = a - hi.astype(F32)
    mid = rest.astype(BF16)
    low = (rest - mid.astype(F32)).astype(BF16)
    return jnp.concatenate([hi, mid, low], axis=0)


def layer_kernel(n, ids_t_ref, ids_ref, gates_ref, hot_tok_ref, hot_gate_ref, x_ref, wg_ref, wu_ref, wd_ref, y_ref,
                 send, recv, out, back, wg, wu, wd, hot_g, hot_u, hot_d, stage_g, stage_u, stage_d,
                 rows_ref, u_ref, fold_ref, weight_ref, acc_ref,
                 load_sem, send_sem, recv_sem, ret_sem, back_sem, from_sem, to_sem):
    me = lax.axis_index('ep')
    devices = 2 * n * n * n
    c, mx, my, mz = me % 2, (me // 2) % n, (me // (2 * n)) % n, me // (2 * n * n)
    blocks = 2 * n * n
    tokens, d_model = x_ref.shape
    d_ff = wd_ref.shape[0]
    top_k = ids_ref.shape[1]
    piece = d_model // FOLD
    main = blocks * SLOTS
    chunk_rows = main + blocks

    def device(z, y, x, core):
        return ((z % n * n + y % n) * n + x % n) * 2 + core % 2

    def peer(q, i, sign):
        kc, kx, ky = i % 2, (i // 2) % n, i // (2 * n)
        kz = (q + 2 * n - kx - ky) % n
        if sign > 0:
            return device(mz + kz, my + ky, mx + kx, c + kc)
        return device(mz + n - kz, my + n - ky, mx + n - kx, c + kc)

    def remote(src, dst, s_sem, r_sem, to):
        return pltpu.make_async_remote_copy(src_ref=src, dst_ref=dst, send_sem=s_sem, recv_sem=r_sem, device_id={'ep': to},
                                            device_id_type=pl.DeviceIdType.MESH)

    def wait_for(ref, sem):
        pltpu.make_async_copy(ref, ref, sem).wait()

    def rows_at(ref, start, size, unit):
        return ref.at[pl.ds(pl.multiple_of(start, unit), size)]

    barrier = pltpu.get_barrier_semaphore()

    @pl.loop(1, devices)
    def _(i):
        pl.semaphore_signal(barrier, inc=1, device_id={'ep': (me + i) % devices}, device_id_type=pl.DeviceIdType.MESH)

    own = [pltpu.make_async_copy(src, dst, load_sem.at[p])
           for p, (src, dst) in enumerate(((wg_ref, wg), (wu_ref, wu), (wd_ref, wd)))]
    for copy in own:
        copy.start()

    unit = d_model // (2 * n * n * n)
    unit_d, unit_c = d_ff // (n * n), d_model // (2 * n)
    parts = ((wg_ref, hot_g, stage_g, mz, (my, mx)), (wu_ref, hot_u, stage_u, mx, (mz, my)), (wd_ref, hot_d, stage_d, my, (mx, mz)))

    def line_device(p, k, core):
        return (device(k, my, mx, core), device(mz, my, k, core), device(mz, k, mx, core))[p]

    def plane_device(p, a, b):
        return (device(mz, a, b, c), device(a, b, mx, c), device(b, my, a, c))[p]

    def quarter(p, ref, half, k):
        if p < 2:
            size = n * n * unit
            return rows_at(ref, half * (d_model // 2) + k * size, size, 16)
        size = n * unit_d
        return ref.at[pl.ds(pl.multiple_of(k * size, 16), size), pl.ds(pl.multiple_of(half * (d_model // 2), 128), d_model // 2)]

    def hot_piece(p, ref, half, k, a, b):
        if p < 2:
            return rows_at(ref, half * (d_model // 2) + k * (n * n * unit) + (a * n + b) * unit, unit, 16)
        return ref.at[pl.ds(pl.multiple_of(k * (n * unit_d) + a * unit_d, 16), unit_d),
                      pl.ds(pl.multiple_of(half * (d_model // 2) + b * unit_c, 128), unit_c)]

    def stage_piece(p, ref, a, b):
        if p < 2:
            return rows_at(ref, (a * n + b) * unit, unit, 16)
        return ref.at[pl.ds(pl.multiple_of(a * unit_d, 16), unit_d), pl.ds(pl.multiple_of(b * unit_c, 128), unit_c)]

    def pieces_like(p, ref):
        if p < 2:
            return ref.at[pl.ds(0, (n * n - 1) * unit)]
        return ref.at[pl.ds(0, (n * n - 1) * unit_d), pl.ds(0, unit_c)]

    def on_line(p):
        plane = parts[p][4]
        return jnp.logical_and(plane[0] == 0, plane[1] == 0)

    def hot_root():
        @pl.when(me == 0)
        def _():
            for p, (src, _, stage, _, _) in enumerate(parts):
                for k in range(n):
                    for half in range(2):
                        if k == 0 and half == 0:
                            pltpu.make_async_copy(quarter(p, src, 0, 0), stage, to_sem.at[0, p]).start()
                        else:
                            remote(quarter(p, src, half, k), stage, from_sem.at[0, p], to_sem.at[0, p], line_device(p, k, half)).start()

    def hot_scatter():
        for p, (_, hot, stage, line, _) in enumerate(parts):
            @pl.when(on_line(p))
            def _(p=p, hot=hot, stage=stage, line=line):
                wait_for(stage, to_sem.at[0, p])

                @pl.loop(1, n * n)
                def _(j):
                    a, b = j // n, j % n
                    remote(stage_piece(p, stage, a, b), hot_piece(p, hot, c, line, a, b), from_sem.at[1, p], to_sem.at[1, p],
                           plane_device(p, a, b)).start()
                hot_piece(p, hot, c, line, 0, 0)[...] = stage_piece(p, stage, 0, 0)[...]

    def hot_plane():
        for p, (_, hot, _, line, plane) in enumerate(parts):
            mine = hot_piece(p, hot, c, line, plane[0], plane[1])

            @pl.when(jnp.logical_not(on_line(p)))
            def _(p=p, mine=mine):
                wait_for(mine, to_sem.at[1, p])

            @pl.loop(1, n * n)
            def _(j, p=p, mine=mine, plane=plane):
                remote(mine, mine, from_sem.at[2, p], to_sem.at[2, p], plane_device(p, plane[0] + j // n, plane[1] + j % n)).start()

    def hot_line():
        for p, (_, hot, _, line, _) in enumerate(parts):
            wait_for(pieces_like(p, hot), to_sem.at[2, p])
            mine = quarter(p, hot, c, line)
            for j in range(1, n):
                remote(mine, mine, from_sem.at[3, p], to_sem.at[3, p], line_device(p, line + j, c)).start()

    def line_like(p, ref):
        if p < 2:
            return ref.at[pl.ds(0, (n - 1) * n * n * unit)]
        return ref.at[pl.ds(0, (n - 1) * n * unit_d), pl.ds(0, d_model // 2)]

    def half_of(p, ref, half):
        if p < 2:
            return rows_at(ref, half * (d_model // 2), d_model // 2, 16)
        return ref.at[:, pl.ds(pl.multiple_of(half * (d_model // 2), 128), d_model // 2)]

    def hot_core():
        for p, (_, hot, _, _, _) in enumerate(parts):
            wait_for(line_like(p, hot), to_sem.at[3, p])
            mine = half_of(p, hot, c)
            remote(mine, mine, from_sem.at[4, p], to_sem.at[4, p], device(mz, my, mx, c + 1)).start()

    def hot_finish():
        for p, (_, hot, _, _, _) in enumerate(parts):
            wait_for(half_of(p, hot, 1 - c), to_sem.at[4, p])
        gate = dotf(x_ref[...], hot_g[...])
        up = dotf(x_ref[...], hot_u[...])
        u = (jax.nn.silu(gate) * up).astype(BF16)
        count = hot_tok_ref.shape[1]
        same = iota((tokens, count), 0) == hot_tok_ref[...]
        weight = jnp.sum(jnp.where(same, hot_gate_ref[...], 0.0), axis=1, keepdims=True)
        is_hot = jnp.sum(jnp.where(same, 1.0, 0.0), axis=1, keepdims=True) > 0.5
        for f in range(FOLD):
            cols = slice(f * piece, (f + 1) * piece)
            h = dotf(u, hot_d[:, cols]).astype(BF16)
            acc_ref[:, cols] = jnp.where(is_hot, weight * h.astype(F32), 0.0)

    def hot_sends_done():
        for p, (src, hot, _, line, _) in enumerate(parts):
            @pl.when(me == 0)
            def _(p=p, src=src):
                if p < 2:
                    wait_for(src.at[pl.ds(0, (2 * n - 1) * n * n * unit)], from_sem.at[0, p])
                else:
                    wait_for(src.at[pl.ds(0, (2 * n - 1) * n * unit_d // 2)], from_sem.at[0, p])

            @pl.when(on_line(p))
            def _(p=p, hot=hot):
                wait_for(pieces_like(p, hot), from_sem.at[1, p])
            wait_for(pieces_like(p, hot), from_sem.at[2, p])
            wait_for(line_like(p, hot), from_sem.at[3, p])
            wait_for(half_of(p, hot, c), from_sem.at[4, p])

    def expert_of(q, i):
        return peer(q, i, 1)

    def fold(pieces):
        r = iota((main, main), 0)
        return dotf(ones_where(iota((main, main), 1) == r % FOLD * blocks + r // FOLD), pieces).astype(BF16)

    def unfold(folded):
        r = iota((main, main), 0)
        return dotf(ones_where(iota((main, main), 1) == r % blocks * FOLD + r // blocks), folded).astype(BF16)

    def pick_rows(q, count, slots):
        row = iota((count, tokens), 0)
        expert = expert_of(q, row // slots)
        member = ids_t_ref[0:1, :] == expert
        for j in range(1, top_k):
            member = jnp.logical_or(member, ids_t_ref[j:j + 1, :] == expert)
        earlier = ones_where(iota((tokens, tokens), 0) < iota((tokens, tokens), 1))
        member_f = jnp.where(member, 1.0, 0.0)
        rank = dotf(member_f.astype(BF16), earlier)
        slot = (row % slots).astype(F32) if slots > 1 else float(SLOTS)
        return jnp.where(rank == slot, member_f, 0.0).astype(BF16)

    def fill(q):
        pick = pick_rows(q, main, SLOTS)
        ninth = pick_rows(q, blocks, 1)
        for f in range(FOLD):
            cols = slice(f * piece, (f + 1) * piece)
            send[q, :, :, cols] = dotf(pick, x_ref[:, cols]).astype(BF16).reshape(blocks, SLOTS, piece)
            fold_ref[f * blocks:(f + 1) * blocks] = dotf(ninth, x_ref[:, cols]).astype(BF16)
        send[q, :, :, d_model:] = fold(fold_ref[...]).reshape(blocks, FOLD, piece)

    def start_sends(q, src, dst, s_sem, r_sem, sign):
        @pl.loop(0, blocks)
        def _(i):
            @pl.when(jnp.logical_or(q > 0, i > 0))
            def _():
                remote(src.at[q, i], dst.at[q, i], s_sem.at[q], r_sem.at[q], peer(q, i, sign)).start()

    def wait_chunk(q, buf, sem):
        @pl.when(q == 0)
        def _():
            wait_for(buf.at[0, pl.ds(1, blocks - 1)], sem.at[0])

        @pl.when(q > 0)
        def _():
            wait_for(buf.at[q], sem.at[q])

    def load_rows(q, buf):
        rows_ref[:main] = buf[q, :, :, :d_model].reshape(main, d_model)
        pieces = unfold(buf[q, :, :, d_model:].reshape(main, piece))
        for f in range(FOLD):
            rows_ref[main:, f * piece:(f + 1) * piece] = pieces[f * blocks:(f + 1) * blocks]

    @pl.loop(0, n)
    def _(q):
        fill(q)

    recv[0, 0] = send[0, 0]
    pl.semaphore_wait(barrier, devices - 1)
    hot_root()

    @pl.loop(0, n)
    def _(q):
        start_sends(q, send, recv, send_sem, recv_sem, 1)

    for copy in own:
        copy.wait()

    width = 256 if d_ff % 256 == 0 else d_ff

    @pl.loop(0, n)
    def _(q):
        wait_chunk(q, recv, recv_sem)
        load_rows(q, recv)
        for w in range(d_ff // width):
            cols = slice(w * width, (w + 1) * width)
            gate = dotf(rows_ref[...], wg[:, cols])
            up = dotf(rows_ref[...], wu[:, cols])
            u_ref[:, cols] = (jax.nn.silu(gate) * up).astype(BF16)
        for f in range(FOLD):
            cols = slice(f * piece, (f + 1) * piece)
            res = dotf(u_ref[...], wd[:, cols]).astype(BF16)
            out[q, :, :, cols] = res[:main].reshape(blocks, SLOTS, piece)
            fold_ref[f * blocks:(f + 1) * blocks] = res[main:]
        out[q, :, :, d_model:] = fold(fold_ref[...]).reshape(blocks, FOLD, piece)
        start_sends(q, out, back, ret_sem, back_sem, -1)

        @pl.when(q == 0)
        def _():
            back[0, 0] = out[0, 0]
            hot_scatter()

        @pl.when(q == 1)
        def _():
            hot_plane()

    hot_line()

    @pl.loop(0, n)
    def _(q):
        def weights(count, slots):
            col = iota((tokens, count), 1)
            expert = expert_of(q, col // slots)
            member = ids_ref[:, 0:1] == expert
            weight = jnp.where(member, gates_ref[:, 0:1], 0.0)
            for j in range(1, top_k):
                here = ids_ref[:, j:j + 1] == expert
                member = jnp.logical_or(member, here)
                weight = jnp.where(here, gates_ref[:, j:j + 1], weight)
            earlier = ones_where(iota((tokens, tokens), 1) < iota((tokens, tokens), 0))
            rank = dotf(earlier, ones_where(member))
            slot = (col % slots).astype(F32) if slots > 1 else float(SLOTS)
            return three_terms(jnp.where(rank == slot, weight, 0.0))
        weight_ref[q, :, :main] = weights(main, SLOTS)
        weight_ref[q, :, main:] = weights(blocks, 1)

    hot_core()
    hot_finish()

    @pl.loop(0, n)
    def _(q):
        wait_chunk(q, back, back_sem)
        load_rows(q, back)
        for f in range(FOLD):
            cols = slice(f * piece, (f + 1) * piece)
            terms = dotf(weight_ref[q], rows_ref[:, cols])
            acc_ref[:, cols] += terms[2 * tokens:] + terms[tokens:2 * tokens] + terms[:tokens]

    y_ref[...] = acc_ref[...].astype(BF16)

    @pl.loop(0, n)
    def _(q):
        wait_chunk(q, send, send_sem)
        wait_chunk(q, out, ret_sem)
    hot_sends_done()


def solution(mesh):
    group_size = mesh.shape['ep']
    n = 1
    while 2 * n * n * n < group_size:
        n += 1
    row_spec = P(('dp', 'ep'), None)
    list_spec = P(('dp', 'ep'))
    expert_spec = P('ep', None, None)

    def local_layer(x, ids, gates, hot_tok, hot_gates, wg, wu, wd):
        wg, wu, wd = wg[0], wu[0], wd[0]
        tokens, d_model = x.shape
        d_ff = wg.shape[1]
        blocks = 2 * n * n
        piece = d_model // FOLD
        main = blocks * SLOTS
        block_buf = pltpu.VMEM((n, blocks, SLOTS, d_model + piece), BF16)
        in_vmem = pl.BlockSpec(memory_space=pltpu.VMEM)
        in_hbm = pl.BlockSpec(memory_space=pl.ANY)
        dma = pltpu.SemaphoreType.DMA
        weights = [pltpu.VMEM((d_model, d_ff), BF16)] * 2 + [pltpu.VMEM((d_ff, d_model), BF16)]
        return pl.pallas_call(
            functools.partial(layer_kernel, n),
            out_shape=jax.ShapeDtypeStruct((tokens, d_model), BF16),
            in_specs=[in_vmem] * 6 + [in_hbm] * 3,
            out_specs=in_vmem,
            scratch_shapes=[block_buf] * 4 + weights + weights
            + [pltpu.VMEM((d_model // (2 * n), d_ff), BF16)] * 2 + [pltpu.VMEM((d_ff // n, d_model // 2), BF16)]
            + [pltpu.VMEM((main + blocks, d_model), BF16), pltpu.VMEM((main + blocks, d_ff), BF16),
               pltpu.VMEM((main, piece), BF16), pltpu.VMEM((n, 3 * tokens, main + blocks), BF16), pltpu.VMEM((tokens, d_model), F32)]
            + [dma((3,)), dma((n,)), dma((n,)), dma((n,)), dma((n,)), dma((5, 3)), dma((5, 3))],
            compiler_params=pltpu.CompilerParams(vmem_limit_bytes=VMEM_LIMIT, collective_id=0, has_side_effects=True),
            name="moe_layer",
        )(ids.T, ids, gates, hot_tok[None, :], hot_gates[None, :], x, wg, wu, wd)

    return jax.shard_map(local_layer, mesh=mesh,
                         in_specs=(row_spec, row_spec, row_spec, list_spec, list_spec, expert_spec, expert_spec, expert_spec),
                         out_specs=row_spec, check_vma=False)
```

time: 1780 us -> 237 us (0.13)
  the two profiles are of different devices: /device:TPU:2 before, /device:TPU:85 now
where the time goes in v2:
time: 237 us
  Pallas kernels  232 us (98%)
  local copies, waits for them, and re-layouts  4.7 us (2%)
    pallas_call x1, Pallas kernels, local_layer(): pl.pallas_call(functools.partial(layer_kernel, n), out_shape=jax.ShapeDty...  232 us

profile of v2, /device:TPU:85, one launch (start us, length us, event | category | flops | bytes accessed | tf_op | source)
XLA Modules:
  0.0 237.0 jit_solution(9507682459669466442)
XLA Ops:
  0.0 1.4 copy.10.gates_ref
  1.4 1.4 copy.9.ids_ref
  2.8 232.3 %moe_layer.1 = bf16[128,2048]{1,0:T(8,128)(2,1)} custom-call(s32[8,128]{1,0:T(8,128)} %bitcast.9, s32[128,8]{1,0:T(8,128)} %copy.9.ids_ref, f32[128,8]{1,0:T(8,128)} %copy.10.gates_ref, s32[1,64]{1,0:T(1,128)} %bitcast.10, f32[1,64]{1,0:T(1,128)} %bitcast.11, bf16[128,2048]{1,0:T(8,128)(2,1)} %x_ref.1, bf16[2048,768]{1,0:T(8,128)(2,1)} %bitcast.6, ...), custom_call_target="tpu_custom_call" | custom-call | tf_op jit(solution)/shard_map/moe_layer/pallas_call | solution.py:369
  235.1 1.9 copy.12

commit v3 on v2

--- a/solution.py
+++ b/solution.py
@@ -34,7 +34,7 @@
     return jnp.concatenate([hi, mid, low], axis=0)
 
 
-def layer_kernel(n, ids_t_ref, ids_ref, gates_ref, hot_tok_ref, hot_gate_ref, x_ref, wg_ref, wu_ref, wd_ref, y_ref,
+def layer_kernel(n, ids_ref, gates_ref, hot_tok_ref, hot_gate_ref, x_ref, wg_ref, wu_ref, wd_ref, y_ref,
                  send, recv, out, back, wg, wu, wd, hot_g, hot_u, hot_d, stage_g, stage_u, stage_d,
                  rows_ref, u_ref, fold_ref, weight_ref, acc_ref,
                  load_sem, send_sem, recv_sem, ret_sem, back_sem, from_sem, to_sem):
@@ -44,7 +44,7 @@
     blocks = 2 * n * n
     tokens, d_model = x_ref.shape
     d_ff = wd_ref.shape[0]
-    top_k = ids_ref.shape[1]
+    top_k = ids_ref.shape[0]
     piece = d_model // FOLD
     main = blocks * SLOTS
     chunk_rows = main + blocks
@@ -221,9 +221,9 @@
     def pick_rows(q, count, slots):
         row = iota((count, tokens), 0)
         expert = expert_of(q, row // slots)
-        member = ids_t_ref[0:1, :] == expert
+        member = ids_ref[0:1, :] == expert
         for j in range(1, top_k):
-            member = jnp.logical_or(member, ids_t_ref[j:j + 1, :] == expert)
+            member = jnp.logical_or(member, ids_ref[j:j + 1, :] == expert)
         earlier = ones_where(iota((tokens, tokens), 0) < iota((tokens, tokens), 1))
         member_f = jnp.where(member, 1.0, 0.0)
         rank = dotf(member_f.astype(BF16), earlier)
@@ -261,26 +261,14 @@
         for f in range(FOLD):
             rows_ref[main:, f * piece:(f + 1) * piece] = pieces[f * blocks:(f + 1) * blocks]
 
-    @pl.loop(0, n)
-    def _(q):
-        fill(q)
-
-    recv[0, 0] = send[0, 0]
-    pl.semaphore_wait(barrier, devices - 1)
-    hot_root()
-
-    @pl.loop(0, n)
-    def _(q):
+    def send_chunk(q):
         start_sends(q, send, recv, send_sem, recv_sem, 1)
 
-    for copy in own:
-        copy.wait()
-
     width = 256 if d_ff % 256 == 0 else d_ff
 
-    @pl.loop(0, n)
-    def _(q):
-        wait_chunk(q, recv, recv_sem)
+    def expert(q):
+        with jax.named_scope("wrecv"):
+            wait_chunk(q, recv, recv_sem)
         load_rows(q, recv)
         for w in range(d_ff // width):
             cols = slice(w * width, (w + 1) * width)
@@ -293,56 +281,91 @@
             out[q, :, :, cols] = res[:main].reshape(blocks, SLOTS, piece)
             fold_ref[f * blocks:(f + 1) * blocks] = res[main:]
         out[q, :, :, d_model:] = fold(fold_ref[...]).reshape(blocks, FOLD, piece)
+
+    def return_chunk(q):
         start_sends(q, out, back, ret_sem, back_sem, -1)
 
-        @pl.when(q == 0)
-        def _():
-            back[0, 0] = out[0, 0]
-            hot_scatter()
-
-        @pl.when(q == 1)
-        def _():
-            hot_plane()
-
-    hot_line()
-
-    @pl.loop(0, n)
-    def _(q):
+    def fill_weights(q):
         def weights(count, slots):
-            col = iota((tokens, count), 1)
-            expert = expert_of(q, col // slots)
-            member = ids_ref[:, 0:1] == expert
-            weight = jnp.where(member, gates_ref[:, 0:1], 0.0)
+            row = iota((count, tokens), 0)
+            expert = expert_of(q, row // slots)
+            member = ids_ref[0:1, :] == expert
+            weight = jnp.where(member, gates_ref[0:1, :], 0.0)
             for j in range(1, top_k):
-                here = ids_ref[:, j:j + 1] == expert
+                here = ids_ref[j:j + 1, :] == expert
                 member = jnp.logical_or(member, here)
-                weight = jnp.where(here, gates_ref[:, j:j + 1], weight)
-            earlier = ones_where(iota((tokens, tokens), 1) < iota((tokens, tokens), 0))
-            rank = dotf(earlier, ones_where(member))
-            slot = (col % slots).astype(F32) if slots > 1 else float(SLOTS)
-            return three_terms(jnp.where(rank == slot, weight, 0.0))
-        weight_ref[q, :, :main] = weights(main, SLOTS)
-        weight_ref[q, :, main:] = weights(blocks, 1)
-
-    hot_core()
-    hot_finish()
-
-    @pl.loop(0, n)
-    def _(q):
-        wait_chunk(q, back, back_sem)
+                weight = jnp.where(here, gates_ref[j:j + 1, :], weight)
+            earlier = ones_where(iota((tokens, tokens), 0) < iota((tokens, tokens), 1))
+            rank = dotf(ones_where(member), earlier)
+            slot = (row % slots).astype(F32) if slots > 1 else float(SLOTS)
+            return jnp.where(rank == slot, weight, 0.0)
+        weight_ref[q, :, :main] = three_terms(weights(main, SLOTS).T)
+        weight_ref[q, :, main:] = three_terms(weights(blocks, 1).T)
+
+    def combine(q):
+        with jax.named_scope("wback"):
+            wait_chunk(q, back, back_sem)
         load_rows(q, back)
         for f in range(FOLD):
             cols = slice(f * piece, (f + 1) * piece)
             terms = dotf(weight_ref[q], rows_ref[:, cols])
             acc_ref[:, cols] += terms[2 * tokens:] + terms[tokens:2 * tokens] + terms[:tokens]
 
+    def fill_step(q):
+        with jax.named_scope("fill"):
+            fill(q)
+
+        @pl.when(q == 0)
+        def _():
+            with jax.named_scope("barrier"):
+                pl.semaphore_wait(barrier, devices - 1)
+            with jax.named_scope("hroot"):
+                hot_root()
+            send_chunk(0)
+
+    pl.loop(0, n)(fill_step)
+    recv[0, 0] = send[0, 0]
+    with jax.named_scope("hscatter"):
+        hot_scatter()
+    send_chunk(1)
+    with jax.named_scope("hplane"):
+        hot_plane()
+    for copy in own:
+        copy.wait()
+
+    with jax.named_scope("send23"):
+        pl.loop(2, n)(send_chunk)
+    with jax.named_scope("fweights"):
+        pl.loop(0, n)(fill_weights)
+
+    @pl.loop(0, n)
+    def _(q):
+        expert(q)
+
+        @pl.when(q == 0)
+        def _():
+            back[0, 0] = out[0, 0]
+            with jax.named_scope("hline"):
+                hot_line()
+
+        return_chunk(q)
+
+        @pl.when(q == n - 1)
+        def _():
+            with jax.named_scope("hcore"):
+                hot_core()
+
+    with jax.named_scope("hfinish"):
+        hot_finish()
+    pl.loop(0, n)(combine)
     y_ref[...] = acc_ref[...].astype(BF16)
 
     @pl.loop(0, n)
     def _(q):
         wait_chunk(q, send, send_sem)
         wait_chunk(q, out, ret_sem)
-    hot_sends_done()
+    with jax.named_scope("hsend"):
+        hot_sends_done()
 
 
 def solution(mesh):
@@ -369,7 +392,7 @@
         return pl.pallas_call(
             functools.partial(layer_kernel, n),
             out_shape=jax.ShapeDtypeStruct((tokens, d_model), BF16),
-            in_specs=[in_vmem] * 6 + [in_hbm] * 3,
+            in_specs=[in_vmem] * 5 + [in_hbm] * 3,
             out_specs=in_vmem,
             scratch_shapes=[block_buf] * 4 + weights + weights
             + [pltpu.VMEM((d_model // (2 * n), d_ff), BF16)] * 2 + [pltpu.VMEM((d_ff // n, d_model // 2), BF16)]
@@ -378,7 +401,7 @@
             + [dma((3,)), dma((n,)), dma((n,)), dma((n,)), dma((n,)), dma((5, 3)), dma((5, 3))],
             compiler_params=pltpu.CompilerParams(vmem_limit_bytes=VMEM_LIMIT, collective_id=0, has_side_effects=True),
             name="moe_layer",
-        )(ids.T, ids, gates, hot_tok[None, :], hot_gates[None, :], x, wg, wu, wd)
+        )(ids.T, gates.T, hot_tok[None, :], hot_gates[None, :], x, wg, wu, wd)
 
     return jax.shard_map(local_layer, mesh=mesh,
                          in_specs=(row_spec, row_spec, row_spec, list_spec, list_spec, expert_spec, expert_spec, expert_spec),

time: 237 us -> 193 us (0.81)
  the two profiles are of different devices: /device:TPU:85 before, /device:TPU:2 now
where the time goes in v3:
time: 193 us
  Pallas kernels  191 us (99%)
    pallas_call x1, Pallas kernels, local_layer(): pl.pallas_call(functools.partial(layer_kernel, n), out_shape=jax.ShapeDty...  191 us

profile of v3, /device:TPU:2, one launch (start us, length us, event | category | flops | bytes accessed | tf_op | source)
XLA Modules:
  0.0 193.1 jit_solution(18438247802701874063)
XLA Ops:
  0.0 191.2 %moe_layer.1 = bf16[128,2048]{1,0:T(8,128)(2,1)} custom-call(s32[8,128]{1,0:T(8,128)} %bitcast.10, f32[8,128]{1,0:T(8,128)} %bitcast.11, s32[1,64]{1,0:T(1,128)} %bitcast.12, f32[1,64]{1,0:T(1,128)} %bitcast.13, bf16[128,2048]{1,0:T(8,128)(2,1)} %x_ref.1, bf16[2048,768]{1,0:T(8,128)(2,1)} %bitcast.7, bf16[2048,768]{1,0:T(8,128)(2,1)} %bitcast.8, ...), custom_call_target="tpu_custom_call" | custom-call | tf_op jit(solution)/shard_map/moe_layer/pallas_call | solution.py:392
  191.2 1.9 copy.10

commit v4 on v3

--- a/solution.py
+++ b/solution.py
@@ -189,7 +189,7 @@
         for f in range(FOLD):
             cols = slice(f * piece, (f + 1) * piece)
             h = dotf(u, hot_d[:, cols]).astype(BF16)
-            acc_ref[:, cols] = jnp.where(is_hot, weight * h.astype(F32), 0.0)
+            acc_ref[:, cols] += jnp.where(is_hot, weight * h.astype(F32), 0.0)
 
     def hot_sends_done():
         for p, (src, hot, _, line, _) in enumerate(parts):
@@ -240,13 +240,15 @@
         send[q, :, :, d_model:] = fold(fold_ref[...]).reshape(blocks, FOLD, piece)
 
     def start_sends(q, src, dst, s_sem, r_sem, sign):
-        @pl.loop(0, blocks)
+        @pl.loop(jnp.where(q == 0, 1, 0) if not isinstance(q, int) else int(q == 0), blocks)
         def _(i):
-            @pl.when(jnp.logical_or(q > 0, i > 0))
-            def _():
-                remote(src.at[q, i], dst.at[q, i], s_sem.at[q], r_sem.at[q], peer(q, i, sign)).start()
+            remote(src.at[q, i], dst.at[q, i], s_sem.at[q], r_sem.at[q], peer(q, i, sign)).start()
 
     def wait_chunk(q, buf, sem):
+        if isinstance(q, int):
+            wait_for(buf.at[0, pl.ds(1, blocks - 1)] if q == 0 else buf.at[q], sem.at[q])
+            return
+
         @pl.when(q == 0)
         def _():
             wait_for(buf.at[0, pl.ds(1, blocks - 1)], sem.at[0])
@@ -302,7 +304,7 @@
         weight_ref[q, :, :main] = three_terms(weights(main, SLOTS).T)
         weight_ref[q, :, main:] = three_terms(weights(blocks, 1).T)
 
-    def combine(q):
+    def add_returned(q):
         with jax.named_scope("wback"):
             wait_chunk(q, back, back_sem)
         load_rows(q, back)
@@ -319,24 +321,19 @@
         def _():
             with jax.named_scope("barrier"):
                 pl.semaphore_wait(barrier, devices - 1)
-            with jax.named_scope("hroot"):
-                hot_root()
+            hot_root()
             send_chunk(0)
 
     pl.loop(0, n)(fill_step)
     recv[0, 0] = send[0, 0]
-    with jax.named_scope("hscatter"):
-        hot_scatter()
-    send_chunk(1)
-    with jax.named_scope("hplane"):
-        hot_plane()
+    acc_ref[...] = jnp.zeros_like(acc_ref)
+    with jax.named_scope("fweights"):
+        pl.loop(0, n)(fill_weights)
     for copy in own:
         copy.wait()
-
-    with jax.named_scope("send23"):
-        pl.loop(2, n)(send_chunk)
-    with jax.named_scope("fweights"):
-        pl.loop(0, n)(fill_weights)
+    with jax.named_scope("wsend0"):
+        wait_chunk(0, send, send_sem)
+    send_chunk(1)
 
     @pl.loop(0, n)
     def _(q):
@@ -345,24 +342,43 @@
         @pl.when(q == 0)
         def _():
             back[0, 0] = out[0, 0]
+
+        return_chunk(q)
+
+        @pl.when(q == 0)
+        def _():
+            with jax.named_scope("hscatter"):
+                hot_scatter()
+
+        @pl.when(q == n // 2 - 1)
+        def _():
+            with jax.named_scope("hplane"):
+                hot_plane()
+
+        @pl.when(q == n // 2)
+        def _():
             with jax.named_scope("hline"):
                 hot_line()
 
-        return_chunk(q)
-
-        @pl.when(q == n - 1)
-        def _():
-            with jax.named_scope("hcore"):
-                hot_core()
-
+        @pl.when(q < n - 2)
+        def _():
+            with jax.named_scope("wsend"):
+                wait_chunk(q + 1, send, send_sem)
+            send_chunk(q + 2)
+
+    pl.loop(0, n // 2)(add_returned)
+    with jax.named_scope("hcore"):
+        hot_core()
+    pl.loop(n // 2, n - 1)(add_returned)
     with jax.named_scope("hfinish"):
         hot_finish()
-    pl.loop(0, n)(combine)
+    add_returned(n - 1)
     y_ref[...] = acc_ref[...].astype(BF16)
+
+    wait_chunk(n - 1, send, send_sem)
 
     @pl.loop(0, n)
     def _(q):
-        wait_chunk(q, send, send_sem)
         wait_chunk(q, out, ret_sem)
     with jax.named_scope("hsend"):
         hot_sends_done()

time: 193 us -> 222 us (1.15)
  Pallas kernels: 191 us -> 220 us
    pallas_call x1, Pallas kernels: 191 us -> 220 us  [local_layer(): pl.pallas_call(functools.partial(layer_kernel, n), out_shape=jax.ShapeDty...]
where the time goes in v4:
time: 222 us
  Pallas kernels  220 us (99%)
    pallas_call x1, Pallas kernels, local_layer(): pl.pallas_call(functools.partial(layer_kernel, n), out_shape=jax.ShapeDty...  220 us

profile of v4, /device:TPU:2, one launch (start us, length us, event | category | flops | bytes accessed | tf_op | source)
XLA Modules:
  0.0 221.6 jit_solution(5900945592149604162)
XLA Ops:
  0.0 219.7 %moe_layer.1 = bf16[128,2048]{1,0:T(8,128)(2,1)} custom-call(s32[8,128]{1,0:T(8,128)} %bitcast.10, f32[8,128]{1,0:T(8,128)} %bitcast.11, s32[1,64]{1,0:T(1,128)} %bitcast.12, f32[1,64]{1,0:T(1,128)} %bitcast.13, bf16[128,2048]{1,0:T(8,128)(2,1)} %x_ref.1, bf16[2048,768]{1,0:T(8,128)(2,1)} %bitcast.7, bf16[2048,768]{1,0:T(8,128)(2,1)} %bitcast.8, ...), custom_call_target="tpu_custom_call" | custom-call | tf_op jit(solution)/shard_map/moe_layer/pallas_call | solution.py:408
  219.7 1.9 copy.10

commit v5 on v4

--- a/solution.py
+++ b/solution.py
@@ -71,9 +71,12 @@
 
     barrier = pltpu.get_barrier_semaphore()
 
-    @pl.loop(1, devices)
-    def _(i):
-        pl.semaphore_signal(barrier, inc=1, device_id={'ep': (me + i) % devices}, device_id_type=pl.DeviceIdType.MESH)
+    def signal_all():
+        @pl.loop(1, devices)
+        def _(i):
+            pl.semaphore_signal(barrier, inc=1, device_id={'ep': (me + i) % devices}, device_id_type=pl.DeviceIdType.MESH)
+
+    pl.when(me != 0)(signal_all)
 
     own = [pltpu.make_async_copy(src, dst, load_sem.at[p])
            for p, (src, dst) in enumerate(((wg_ref, wg), (wu_ref, wu), (wd_ref, wd)))]
@@ -82,7 +85,7 @@
 
     unit = d_model // (2 * n * n * n)
     unit_d, unit_c = d_ff // (n * n), d_model // (2 * n)
-    parts = ((wg_ref, hot_g, stage_g, mz, (my, mx)), (wu_ref, hot_u, stage_u, mx, (mz, my)), (wd_ref, hot_d, stage_d, my, (mx, mz)))
+    parts = ((wg, hot_g, stage_g, mz, (my, mx)), (wu, hot_u, stage_u, mx, (mz, my)), (wd, hot_d, stage_d, my, (mx, mz)))
 
     def line_device(p, k, core):
         return (device(k, my, mx, core), device(mz, my, k, core), device(mz, k, mx, core))[p]
@@ -118,21 +121,27 @@
         return jnp.logical_and(plane[0] == 0, plane[1] == 0)
 
     def hot_root():
-        @pl.when(me == 0)
-        def _():
-            for p, (src, _, stage, _, _) in enumerate(parts):
-                for k in range(n):
-                    for half in range(2):
-                        if k == 0 and half == 0:
-                            pltpu.make_async_copy(quarter(p, src, 0, 0), stage, to_sem.at[0, p]).start()
-                        else:
-                            remote(quarter(p, src, half, k), stage, from_sem.at[0, p], to_sem.at[0, p], line_device(p, k, half)).start()
+        for copy in own:
+            copy.wait()
+        pl.semaphore_wait(barrier, devices - 1)
+        for k in (*range(n // 2, 0, -1), *range(n - 1, n // 2, -1), 0):
+            for half in range(2):
+                for p, (src, _, stage, _, _) in enumerate(parts):
+                    if k > 0 or half > 0:
+                        remote(quarter(p, src, half, k), stage, from_sem.at[0, p], to_sem.at[0, p], line_device(p, k, half)).start()
+        for p, (src, _, stage, _, _) in enumerate(parts):
+            stage[...] = quarter(p, src, 0, 0)[...]
+        for p, (src, _, _, _, _) in enumerate(parts):
+            wait_for(src.at[pl.ds(0, (2 * n - 1) * (n * n * unit if p < 2 else n * unit_d // 2))], from_sem.at[0, p])
+        signal_all()
 
     def hot_scatter():
         for p, (_, hot, stage, line, _) in enumerate(parts):
             @pl.when(on_line(p))
             def _(p=p, hot=hot, stage=stage, line=line):
-                wait_for(stage, to_sem.at[0, p])
+                @pl.when(me != 0)
+                def _():
+                    wait_for(stage, to_sem.at[0, p])
 
                 @pl.loop(1, n * n)
                 def _(j):
@@ -192,14 +201,7 @@
             acc_ref[:, cols] += jnp.where(is_hot, weight * h.astype(F32), 0.0)
 
     def hot_sends_done():
-        for p, (src, hot, _, line, _) in enumerate(parts):
-            @pl.when(me == 0)
-            def _(p=p, src=src):
-                if p < 2:
-                    wait_for(src.at[pl.ds(0, (2 * n - 1) * n * n * unit)], from_sem.at[0, p])
-                else:
-                    wait_for(src.at[pl.ds(0, (2 * n - 1) * n * unit_d // 2)], from_sem.at[0, p])
-
+        for p, (_, hot, _, _, _) in enumerate(parts):
             @pl.when(on_line(p))
             def _(p=p, hot=hot):
                 wait_for(pieces_like(p, hot), from_sem.at[1, p])
@@ -313,27 +315,27 @@
             terms = dotf(weight_ref[q], rows_ref[:, cols])
             acc_ref[:, cols] += terms[2 * tokens:] + terms[tokens:2 * tokens] + terms[:tokens]
 
-    def fill_step(q):
-        with jax.named_scope("fill"):
-            fill(q)
-
-        @pl.when(q == 0)
-        def _():
-            with jax.named_scope("barrier"):
-                pl.semaphore_wait(barrier, devices - 1)
-            hot_root()
-            send_chunk(0)
-
-    pl.loop(0, n)(fill_step)
+    def others_wait():
+        for copy in own:
+            copy.wait()
+        pl.semaphore_wait(barrier, devices - 1)
+
+    with jax.named_scope("fill"):
+        pl.loop(0, n)(fill)
     recv[0, 0] = send[0, 0]
     acc_ref[...] = jnp.zeros_like(acc_ref)
+    with jax.named_scope("root"):
+        pl.when(me == 0)(hot_root)
+    with jax.named_scope("barrier"):
+        pl.when(me != 0)(others_wait)
+    with jax.named_scope("hscatter"):
+        hot_scatter()
+    send_chunk(0)
+    with jax.named_scope("hplane"):
+        hot_plane()
+    send_chunk(1)
     with jax.named_scope("fweights"):
         pl.loop(0, n)(fill_weights)
-    for copy in own:
-        copy.wait()
-    with jax.named_scope("wsend0"):
-        wait_chunk(0, send, send_sem)
-    send_chunk(1)
 
     @pl.loop(0, n)
     def _(q):
@@ -342,28 +344,13 @@
         @pl.when(q == 0)
         def _():
             back[0, 0] = out[0, 0]
-
-        return_chunk(q)
-
-        @pl.when(q == 0)
-        def _():
-            with jax.named_scope("hscatter"):
-                hot_scatter()
-
-        @pl.when(q == n // 2 - 1)
-        def _():
-            with jax.named_scope("hplane"):
-                hot_plane()
-
-        @pl.when(q == n // 2)
-        def _():
             with jax.named_scope("hline"):
                 hot_line()
 
+        return_chunk(q)
+
         @pl.when(q < n - 2)
         def _():
-            with jax.named_scope("wsend"):
-                wait_chunk(q + 1, send, send_sem)
             send_chunk(q + 2)
 
     pl.loop(0, n // 2)(add_returned)
@@ -375,10 +362,9 @@
     add_returned(n - 1)
     y_ref[...] = acc_ref[...].astype(BF16)
 
-    wait_chunk(n - 1, send, send_sem)
-
     @pl.loop(0, n)
     def _(q):
+        wait_chunk(q, send, send_sem)
         wait_chunk(q, out, ret_sem)
     with jax.named_scope("hsend"):
         hot_sends_done()

time: 222 us -> 207 us (0.932)
  the two profiles are of different devices: /device:TPU:2 before, /device:TPU:19 now
where the time goes in v5:
time: 207 us; the launch traced here: 206 us
  Pallas kernels  205 us (99%)
    pallas_call x1, Pallas kernels, local_layer(): pl.pallas_call(functools.partial(layer_kernel, n), out_shape=jax.ShapeDty...  205 us

profile of v5, /device:TPU:19, one launch (start us, length us, event | category | flops | bytes accessed | tf_op | source)
XLA Modules:
  0.0 206.4 jit_solution(8394949294446963197)
XLA Ops:
  0.0 204.5 %moe_layer.1 = bf16[128,2048]{1,0:T(8,128)(2,1)} custom-call(s32[8,128]{1,0:T(8,128)} %bitcast.10, f32[8,128]{1,0:T(8,128)} %bitcast.11, s32[1,64]{1,0:T(1,128)} %bitcast.12, f32[1,64]{1,0:T(1,128)} %bitcast.13, bf16[128,2048]{1,0:T(8,128)(2,1)} %x_ref.1, bf16[2048,768]{1,0:T(8,128)(2,1)} %bitcast.7, bf16[2048,768]{1,0:T(8,128)(2,1)} %bitcast.8, ...), custom_call_target="tpu_custom_call" | custom-call | tf_op jit(solution)/shard_map/moe_layer/pallas_call | solution.py:394
  204.5 1.9 copy.10

commit v6 on v5

--- a/solution.py
+++ b/solution.py
@@ -35,9 +35,9 @@
 
 
 def layer_kernel(n, ids_ref, gates_ref, hot_tok_ref, hot_gate_ref, x_ref, wg_ref, wu_ref, wd_ref, y_ref,
-                 send, recv, out, back, wg, wu, wd, hot_g, hot_u, hot_d, stage_g, stage_u, stage_d,
+                 send, recv, out, back, relay_out, relay_back, wg, wu, wd, hot_g, hot_u, hot_d, stage_g, stage_u, stage_d,
                  rows_ref, u_ref, fold_ref, weight_ref, acc_ref,
-                 load_sem, send_sem, recv_sem, ret_sem, back_sem, from_sem, to_sem):
+                 load_sem, send_sem, recv_sem, ret_sem, back_sem, mid_sem, on_sem, from_sem, to_sem):
     me = lax.axis_index('ep')
     devices = 2 * n * n * n
     c, mx, my, mz = me % 2, (me // 2) % n, (me // (2 * n)) % n, me // (2 * n * n)
@@ -52,12 +52,36 @@
     def device(z, y, x, core):
         return ((z % n * n + y % n) * n + x % n) * 2 + core % 2
 
+    def steps(q, i):
+        kx, ky = (i // 2) % n, i // (2 * n)
+        return i % 2, kx, ky, (q + 2 * n - kx - ky) % n
+
     def peer(q, i, sign):
-        kc, kx, ky = i % 2, (i // 2) % n, i // (2 * n)
-        kz = (q + 2 * n - kx - ky) % n
+        kc, kx, ky, kz = steps(q, i)
         if sign > 0:
             return device(mz + kz, my + ky, mx + kx, c + kc)
         return device(mz + n - kz, my + n - ky, mx + n - kx, c + kc)
+
+    relayed = n == 4
+
+    def opposite(k):
+        return k == n // 2
+
+    def is_relayed(q, i):
+        _, kx, ky, kz = steps(q, i)
+        return jnp.logical_or(jnp.logical_or(opposite(kx), opposite(ky)), opposite(kz))
+
+    def relay_count(q):
+        pairs = [(kx, ky) for kx in range(n) for ky in range(n)]
+        return 2 * sum(kx == n // 2 or ky == n // 2 or (q - kx - ky) % n == n // 2 for kx, ky in pairs)
+
+    def hop(q, i, sign, leg):
+        kc, kx, ky, kz = steps(q, i)
+        way = jnp.where(kc == 0, 1, n - 1)
+        move = [jnp.where(opposite(k), way, k if leg == 0 else 0) for k in (kz, ky, kx)]
+        if sign < 0:
+            move = [n - m for m in move]
+        return device(mz + move[0], my + move[1], mx + move[2], c + kc if leg == 0 else c)
 
     def remote(src, dst, s_sem, r_sem, to):
         return pltpu.make_async_remote_copy(src_ref=src, dst_ref=dst, send_sem=s_sem, recv_sem=r_sem, device_id={'ep': to},
@@ -162,17 +186,35 @@
             def _(j, p=p, mine=mine, plane=plane):
                 remote(mine, mine, from_sem.at[2, p], to_sem.at[2, p], plane_device(p, plane[0] + j // n, plane[1] + j % n)).start()
 
+    def part_of_quarter(p, ref, half, k, which):
+        if p < 2:
+            size = n * n * unit // 2
+            return rows_at(ref, half * (d_model // 2) + (2 * k + which) * size, size, 16)
+        size = n * unit_d // 2
+        return ref.at[pl.ds(pl.multiple_of((2 * k + which) * size, 16), size), pl.ds(pl.multiple_of(half * (d_model // 2), 128), d_model // 2)]
+
     def hot_line():
         for p, (_, hot, _, line, _) in enumerate(parts):
             wait_for(pieces_like(p, hot), to_sem.at[2, p])
             mine = quarter(p, hot, c, line)
-            for j in range(1, n):
-                remote(mine, mine, from_sem.at[3, p], to_sem.at[3, p], line_device(p, line + j, c)).start()
-
-    def line_like(p, ref):
-        if p < 2:
-            return ref.at[pl.ds(0, (n - 1) * n * n * unit)]
-        return ref.at[pl.ds(0, (n - 1) * n * unit_d), pl.ds(0, d_model // 2)]
+            remote(mine, mine, from_sem.at[3, p], to_sem.at[3, p], line_device(p, line + 1, c)).start()
+            if n > 2:
+                remote(mine, mine, from_sem.at[3, p], to_sem.at[3, p], line_device(p, line + n - 1, c)).start()
+
+    def hot_opposite():
+        for p, (_, hot, _, line, _) in enumerate(parts):
+            wait_for(neighbours_like(p, hot), to_sem.at[3, p])
+            if n > 2:
+                first = part_of_quarter(p, hot, c, (line + n - 1) % n, 0)
+                second = part_of_quarter(p, hot, c, (line + 1) % n, 1)
+                remote(first, first, from_sem.at[5, p], to_sem.at[5, p], line_device(p, line + 1, c)).start()
+                remote(second, second, from_sem.at[5, p], to_sem.at[5, p], line_device(p, line + n - 1, c)).start()
+
+    def neighbours_like(p, ref):
+        count = min(2, n - 1)
+        if p < 2:
+            return ref.at[pl.ds(0, count * n * n * unit)]
+        return ref.at[pl.ds(0, count * n * unit_d), pl.ds(0, d_model // 2)]
 
     def half_of(p, ref, half):
         if p < 2:
@@ -181,7 +223,8 @@
 
     def hot_core():
         for p, (_, hot, _, _, _) in enumerate(parts):
-            wait_for(line_like(p, hot), to_sem.at[3, p])
+            if n > 2:
+                wait_for(quarter(p, hot, c, 0), to_sem.at[5, p])
             mine = half_of(p, hot, c)
             remote(mine, mine, from_sem.at[4, p], to_sem.at[4, p], device(mz, my, mx, c + 1)).start()
 
@@ -206,7 +249,9 @@
             def _(p=p, hot=hot):
                 wait_for(pieces_like(p, hot), from_sem.at[1, p])
             wait_for(pieces_like(p, hot), from_sem.at[2, p])
-            wait_for(line_like(p, hot), from_sem.at[3, p])
+            wait_for(neighbours_like(p, hot), from_sem.at[3, p])
+            if n > 2:
+                wait_for(quarter(p, hot, c, 0), from_sem.at[5, p])
             wait_for(half_of(p, hot, c), from_sem.at[4, p])
 
     def expert_of(q, i):
@@ -241,10 +286,53 @@
             fold_ref[f * blocks:(f + 1) * blocks] = dotf(ninth, x_ref[:, cols]).astype(BF16)
         send[q, :, :, d_model:] = fold(fold_ref[...]).reshape(blocks, FOLD, piece)
 
-    def start_sends(q, src, dst, s_sem, r_sem, sign):
-        @pl.loop(jnp.where(q == 0, 1, 0) if not isinstance(q, int) else int(q == 0), blocks)
+    def start_sends(q, src, dst, relay, way, s_sem, r_sem, sign):
+        first = int(q == 0) if isinstance(q, int) else jnp.where(q == 0, 1, 0)
+        if relayed:
+            @pl.loop(0, blocks)
+            def _(i):
+                @pl.when(is_relayed(q, i))
+                def _():
+                    remote(src.at[q, i], relay.at[q, i], s_sem.at[q], mid_sem.at[way, q], hop(q, i, sign, 0)).start()
+
+        @pl.loop(first, blocks)
         def _(i):
-            remote(src.at[q, i], dst.at[q, i], s_sem.at[q], r_sem.at[q], peer(q, i, sign)).start()
+            def direct():
+                remote(src.at[q, i], dst.at[q, i], s_sem.at[q], r_sem.at[q], peer(q, i, sign)).start()
+            if relayed:
+                pl.when(jnp.logical_not(is_relayed(q, i)))(direct)
+            else:
+                direct()
+
+    def wait_relay(q, relay, sem):
+        for count in sorted({relay_count(k) for k in range(n)}):
+            chunks = [k for k in range(n) if relay_count(k) == count]
+            if isinstance(q, int):
+                if q in chunks:
+                    wait_for(relay.at[q, pl.ds(0, count)], sem)
+            else:
+                same = functools.reduce(jnp.logical_or, [q == k for k in chunks])
+
+                @pl.when(same)
+                def _(count=count):
+                    wait_for(relay.at[q, pl.ds(0, count)], sem)
+
+    def pass_on(q, dst, relay, way, r_sem, sign):
+        if not relayed:
+            return
+        wait_relay(q, relay, mid_sem.at[way, q])
+
+        @pl.loop(0, blocks)
+        def _(i):
+            @pl.when(is_relayed(q, i))
+            def _():
+                remote(relay.at[q, i], dst.at[q, i], on_sem.at[way, q], r_sem.at[q], hop(q, i, sign, 1)).start()
+
+    def pass_on_sent(q):
+        pass_on(q, recv, relay_out, 0, recv_sem, 1)
+
+    def pass_on_returned(q):
+        pass_on(q, back, relay_back, 1, back_sem, -1)
 
     def wait_chunk(q, buf, sem):
         if isinstance(q, int):
@@ -266,7 +354,7 @@
             rows_ref[main:, f * piece:(f + 1) * piece] = pieces[f * blocks:(f + 1) * blocks]
 
     def send_chunk(q):
-        start_sends(q, send, recv, send_sem, recv_sem, 1)
+        start_sends(q, send, recv, relay_out, 0, send_sem, recv_sem, 1)
 
     width = 256 if d_ff % 256 == 0 else d_ff
 
@@ -287,7 +375,7 @@
         out[q, :, :, d_model:] = fold(fold_ref[...]).reshape(blocks, FOLD, piece)
 
     def return_chunk(q):
-        start_sends(q, out, back, ret_sem, back_sem, -1)
+        start_sends(q, out, back, relay_back, 1, ret_sem, back_sem, -1)
 
     def fill_weights(q):
         def weights(count, slots):
@@ -336,6 +424,8 @@
     send_chunk(1)
     with jax.named_scope("fweights"):
         pl.loop(0, n)(fill_weights)
+    with jax.named_scope("psent0"):
+        pass_on_sent(0)
 
     @pl.loop(0, n)
     def _(q):
@@ -344,18 +434,38 @@
         @pl.when(q == 0)
         def _():
             back[0, 0] = out[0, 0]
+
+        return_chunk(q)
+
+        @pl.when(q < n - 1)
+        def _():
+            with jax.named_scope("psent"):
+                pass_on_sent(q + 1)
+
+        @pl.when(q < n - 2)
+        def _():
+            send_chunk(q + 2)
+
+        @pl.when(q > 0)
+        def _():
+            with jax.named_scope("pret"):
+                pass_on_returned(q - 1)
+
+        @pl.when(q == 0)
+        def _():
             with jax.named_scope("hline"):
                 hot_line()
 
-        return_chunk(q)
-
-        @pl.when(q < n - 2)
-        def _():
-            send_chunk(q + 2)
-
-    pl.loop(0, n // 2)(add_returned)
+        @pl.when(q == 1)
+        def _():
+            with jax.named_scope("hopp"):
+                hot_opposite()
+
     with jax.named_scope("hcore"):
         hot_core()
+    pl.loop(0, n // 2)(add_returned)
+    with jax.named_scope("pretlast"):
+        pass_on_returned(n - 1)
     pl.loop(n // 2, n - 1)(add_returned)
     with jax.named_scope("hfinish"):
         hot_finish()
@@ -366,6 +476,9 @@
     def _(q):
         wait_chunk(q, send, send_sem)
         wait_chunk(q, out, ret_sem)
+        if relayed:
+            wait_relay(q, relay_out, on_sem.at[0, q])
+            wait_relay(q, relay_back, on_sem.at[1, q])
     with jax.named_scope("hsend"):
         hot_sends_done()
 
@@ -396,11 +509,11 @@
             out_shape=jax.ShapeDtypeStruct((tokens, d_model), BF16),
             in_specs=[in_vmem] * 5 + [in_hbm] * 3,
             out_specs=in_vmem,
-            scratch_shapes=[block_buf] * 4 + weights + weights
+            scratch_shapes=[block_buf] * 6 + weights + weights
             + [pltpu.VMEM((d_model // (2 * n), d_ff), BF16)] * 2 + [pltpu.VMEM((d_ff // n, d_model // 2), BF16)]
             + [pltpu.VMEM((main + blocks, d_model), BF16), pltpu.VMEM((main + blocks, d_ff), BF16),
                pltpu.VMEM((main, piece), BF16), pltpu.VMEM((n, 3 * tokens, main + blocks), BF16), pltpu.VMEM((tokens, d_model), F32)]
-            + [dma((3,)), dma((n,)), dma((n,)), dma((n,)), dma((n,)), dma((5, 3)), dma((5, 3))],
+            + [dma((3,)), dma((n,)), dma((n,)), dma((n,)), dma((n,)), dma((2, n)), dma((2, n)), dma((6, 3)), dma((6, 3))],
             compiler_params=pltpu.CompilerParams(vmem_limit_bytes=VMEM_LIMIT, collective_id=0, has_side_effects=True),
             name="moe_layer",
         )(ids.T, gates.T, hot_tok[None, :], hot_gates[None, :], x, wg, wu, wd)

time: 207 us -> 178 us (0.86)
  the two profiles are of different devices: /device:TPU:19 before, /device:TPU:2 now
where the time goes in v6:
time: 178 us
  Pallas kernels  176 us (99%)
  local copies, waits for them, and re-layouts  1.88 us (1%)
    pallas_call x1, Pallas kernels, local_layer(): pl.pallas_call(functools.partial(layer_kernel, n), out_shape=jax.ShapeDty...  176 us

profile of v6, /device:TPU:2, one launch (start us, length us, event | category | flops | bytes accessed | tf_op | source)
XLA Modules:
  0.0 177.6 jit_solution(2981851028187886225)
XLA Ops:
  0.0 175.7 %moe_layer.1 = bf16[128,2048]{1,0:T(8,128)(2,1)} custom-call(s32[8,128]{1,0:T(8,128)} %bitcast.10, f32[8,128]{1,0:T(8,128)} %bitcast.11, s32[1,64]{1,0:T(1,128)} %bitcast.12, f32[1,64]{1,0:T(1,128)} %bitcast.13, bf16[128,2048]{1,0:T(8,128)(2,1)} %x_ref.1, bf16[2048,768]{1,0:T(8,128)(2,1)} %bitcast.7, bf16[2048,768]{1,0:T(8,128)(2,1)} %bitcast.8, ...), custom_call_target="tpu_custom_call" | custom-call | tf_op jit(solution)/shard_map/moe_layer/pallas_call | solution.py:507
  175.7 1.9 %copy.10 = bf16[128,2048]{1,0:T(8,128)(2,1)} copy(bf16[128,2048]{1,0:T(8,128)(2,1)} %moe_layer.1) | data formatting | bytes 1048576

commit v7 on v6

--- a/solution.py
+++ b/solution.py
@@ -12,6 +12,9 @@
 SLOTS = 8
 FOLD = 8
 VMEM_LIMIT = 60 * 1024 * 1024
+SPLIT = 2
+AHEAD = 6
+LEAD = 2
 
 
 def dotf(a, b):
@@ -41,7 +44,8 @@
     me = lax.axis_index('ep')
     devices = 2 * n * n * n
     c, mx, my, mz = me % 2, (me // 2) % n, (me // (2 * n)) % n, me // (2 * n * n)
-    blocks = 2 * n * n
+    chunks = SPLIT * n
+    blocks = 2 * n * n // SPLIT
     tokens, d_model = x_ref.shape
     d_ff = wd_ref.shape[0]
     top_k = ids_ref.shape[0]
@@ -53,8 +57,8 @@
         return ((z % n * n + y % n) * n + x % n) * 2 + core % 2
 
     def steps(q, i):
-        kx, ky = (i // 2) % n, i // (2 * n)
-        return i % 2, kx, ky, (q + 2 * n - kx - ky) % n
+        kx, ky = (i // 2) % n, i // (2 * n) * SPLIT + q % SPLIT
+        return i % 2, kx, ky, (q // SPLIT + 2 * n - kx - ky) % n
 
     def peer(q, i, sign):
         kc, kx, ky, kz = steps(q, i)
@@ -72,8 +76,7 @@
         return jnp.logical_or(jnp.logical_or(opposite(kx), opposite(ky)), opposite(kz))
 
     def relay_count(q):
-        pairs = [(kx, ky) for kx in range(n) for ky in range(n)]
-        return 2 * sum(kx == n // 2 or ky == n // 2 or (q - kx - ky) % n == n // 2 for kx, ky in pairs)
+        return sum(any(opposite(k) for k in steps(q, i)[1:]) for i in range(blocks))
 
     def hop(q, i, sign, leg):
         kc, kx, ky, kz = steps(q, i)
@@ -144,19 +147,24 @@
         plane = parts[p][4]
         return jnp.logical_and(plane[0] == 0, plane[1] == 0)
 
+    def sent_like(late):
+        count = 1 if late else 2 * n - 2
+        for p, (src, _, _, _, _) in enumerate(parts):
+            wait_for(src.at[pl.ds(0, count * (n * n * unit if p < 2 else n * unit_d // 2))], from_sem.at[6 * late, p])
+
     def hot_root():
         for copy in own:
             copy.wait()
         pl.semaphore_wait(barrier, devices - 1)
-        for k in (*range(n // 2, 0, -1), *range(n - 1, n // 2, -1), 0):
-            for half in range(2):
-                for p, (src, _, stage, _, _) in enumerate(parts):
-                    if k > 0 or half > 0:
-                        remote(quarter(p, src, half, k), stage, from_sem.at[0, p], to_sem.at[0, p], line_device(p, k, half)).start()
+        order = [(k, half) for k in (*range(n // 2, n), 0, *range(n // 2 - 1, 0, -1)) for half in range(2)]
+        for k, half in order:
+            for p, (src, _, stage, _, _) in enumerate(parts):
+                if k > 0 or half > 0:
+                    remote(quarter(p, src, half, k), stage, from_sem.at[0 if (k, half) != order[-1] else 6, p], to_sem.at[0, p],
+                           line_device(p, k, half)).start()
         for p, (src, _, stage, _, _) in enumerate(parts):
             stage[...] = quarter(p, src, 0, 0)[...]
-        for p, (src, _, _, _, _) in enumerate(parts):
-            wait_for(src.at[pl.ds(0, (2 * n - 1) * (n * n * unit if p < 2 else n * unit_d // 2))], from_sem.at[0, p])
+        sent_like(0)
         signal_all()
 
     def hot_scatter():
@@ -244,10 +252,15 @@
             acc_ref[:, cols] += jnp.where(is_hot, weight * h.astype(F32), 0.0)
 
     def hot_sends_done():
+        @pl.when(me == 0)
+        def _():
+            sent_like(1)
+
         for p, (_, hot, _, _, _) in enumerate(parts):
             @pl.when(on_line(p))
             def _(p=p, hot=hot):
                 wait_for(pieces_like(p, hot), from_sem.at[1, p])
+
             wait_for(pieces_like(p, hot), from_sem.at[2, p])
             wait_for(neighbours_like(p, hot), from_sem.at[3, p])
             if n > 2:
@@ -305,13 +318,13 @@
                 direct()
 
     def wait_relay(q, relay, sem):
-        for count in sorted({relay_count(k) for k in range(n)}):
-            chunks = [k for k in range(n) if relay_count(k) == count]
+        for count in sorted({relay_count(k) for k in range(chunks)}):
+            alike = [k for k in range(chunks) if relay_count(k) == count]
             if isinstance(q, int):
-                if q in chunks:
+                if q in alike:
                     wait_for(relay.at[q, pl.ds(0, count)], sem)
             else:
-                same = functools.reduce(jnp.logical_or, [q == k for k in chunks])
+                same = functools.reduce(jnp.logical_or, [q == k for k in alike])
 
                 @pl.when(same)
                 def _(count=count):
@@ -409,7 +422,7 @@
         pl.semaphore_wait(barrier, devices - 1)
 
     with jax.named_scope("fill"):
-        pl.loop(0, n)(fill)
+        pl.loop(0, chunks)(fill)
     recv[0, 0] = send[0, 0]
     acc_ref[...] = jnp.zeros_like(acc_ref)
     with jax.named_scope("root"):
@@ -418,17 +431,23 @@
         pl.when(me != 0)(others_wait)
     with jax.named_scope("hscatter"):
         hot_scatter()
-    send_chunk(0)
+    ahead = min(AHEAD, chunks)
+    pl.loop(0, LEAD)(send_chunk)
     with jax.named_scope("hplane"):
         hot_plane()
-    send_chunk(1)
+    pl.loop(LEAD, ahead)(send_chunk)
     with jax.named_scope("fweights"):
-        pl.loop(0, n)(fill_weights)
+        pl.loop(0, chunks)(fill_weights)
     with jax.named_scope("psent0"):
-        pass_on_sent(0)
-
-    @pl.loop(0, n)
+        pl.loop(0, LEAD)(pass_on_sent)
+
+    @pl.loop(0, chunks)
     def _(q):
+        @pl.when(q < chunks - LEAD)
+        def _():
+            with jax.named_scope("psent"):
+                pass_on_sent(q + LEAD)
+
         expert(q)
 
         @pl.when(q == 0)
@@ -437,42 +456,37 @@
 
         return_chunk(q)
 
-        @pl.when(q < n - 1)
-        def _():
-            with jax.named_scope("psent"):
-                pass_on_sent(q + 1)
-
-        @pl.when(q < n - 2)
-        def _():
-            send_chunk(q + 2)
+        @pl.when(q < chunks - ahead)
+        def _():
+            send_chunk(q + ahead)
 
         @pl.when(q > 0)
         def _():
             with jax.named_scope("pret"):
                 pass_on_returned(q - 1)
 
-        @pl.when(q == 0)
+        @pl.when(q == 1)
         def _():
             with jax.named_scope("hline"):
                 hot_line()
 
-        @pl.when(q == 1)
+        @pl.when(q == chunks // 2)
         def _():
             with jax.named_scope("hopp"):
                 hot_opposite()
 
     with jax.named_scope("hcore"):
         hot_core()
-    pl.loop(0, n // 2)(add_returned)
+    pl.loop(0, chunks // 2)(add_returned)
     with jax.named_scope("pretlast"):
-        pass_on_returned(n - 1)
-    pl.loop(n // 2, n - 1)(add_returned)
+        pass_on_returned(chunks - 1)
+    pl.loop(chunks // 2, chunks - 1)(add_returned)
     with jax.named_scope("hfinish"):
         hot_finish()
-    add_returned(n - 1)
+    add_returned(chunks - 1)
     y_ref[...] = acc_ref[...].astype(BF16)
 
-    @pl.loop(0, n)
+    @pl.loop(0, chunks)
     def _(q):
         wait_chunk(q, send, send_sem)
         wait_chunk(q, out, ret_sem)
@@ -496,10 +510,11 @@
         wg, wu, wd = wg[0], wu[0], wd[0]
         tokens, d_model = x.shape
         d_ff = wg.shape[1]
-        blocks = 2 * n * n
+        chunks = SPLIT * n
+        blocks = 2 * n * n // SPLIT
         piece = d_model // FOLD
         main = blocks * SLOTS
-        block_buf = pltpu.VMEM((n, blocks, SLOTS, d_model + piece), BF16)
+        block_buf = pltpu.VMEM((chunks, blocks, SLOTS, d_model + piece), BF16)
         in_vmem = pl.BlockSpec(memory_space=pltpu.VMEM)
         in_hbm = pl.BlockSpec(memory_space=pl.ANY)
         dma = pltpu.SemaphoreType.DMA
@@ -512,8 +527,8 @@
             scratch_shapes=[block_buf] * 6 + weights + weights
             + [pltpu.VMEM((d_model // (2 * n), d_ff), BF16)] * 2 + [pltpu.VMEM((d_ff // n, d_model // 2), BF16)]
             + [pltpu.VMEM((main + blocks, d_model), BF16), pltpu.VMEM((main + blocks, d_ff), BF16),
-               pltpu.VMEM((main, piece), BF16), pltpu.VMEM((n, 3 * tokens, main + blocks), BF16), pltpu.VMEM((tokens, d_model), F32)]
-            + [dma((3,)), dma((n,)), dma((n,)), dma((n,)), dma((n,)), dma((2, n)), dma((2, n)), dma((6, 3)), dma((6, 3))],
+               pltpu.VMEM((main, piece), BF16), pltpu.VMEM((chunks, 3 * tokens, main + blocks), BF16), pltpu.VMEM((tokens, d_model), F32)]
+            + [dma((3,))] + [dma((chunks,))] * 4 + [dma((2, chunks))] * 2 + [dma((7, 3)), dma((6, 3))],
             compiler_params=pltpu.CompilerParams(vmem_limit_bytes=VMEM_LIMIT, collective_id=0, has_side_effects=True),
             name="moe_layer",
         )(ids.T, gates.T, hot_tok[None, :], hot_gates[None, :], x, wg, wu, wd)

time: 178 us -> 176 us (0.989)
  the two profiles are of different devices: /device:TPU:2 before, /device:TPU:1 now
where the time goes in v7:
time: 176 us
  Pallas kernels  174 us (99%)
  local copies, waits for them, and re-layouts  1.88 us (1%)
    pallas_call x1, Pallas kernels, local_layer(): pl.pallas_call(functools.partial(layer_kernel, n), out_shape=jax.ShapeDty...  174 us

profile of v7, /device:TPU:1, one launch (start us, length us, event | category | flops | bytes accessed | tf_op | source)
XLA Modules:
  0.0 175.9 jit_solution(2130225608455955926)
XLA Ops:
  0.0 174.0 %moe_layer.1 = bf16[128,2048]{1,0:T(8,128)(2,1)} custom-call(s32[8,128]{1,0:T(8,128)} %bitcast.10, f32[8,128]{1,0:T(8,128)} %bitcast.11, s32[1,64]{1,0:T(1,128)} %bitcast.12, f32[1,64]{1,0:T(1,128)} %bitcast.13, bf16[128,2048]{1,0:T(8,128)(2,1)} %x_ref.1, bf16[2048,768]{1,0:T(8,128)(2,1)} %bitcast.7, bf16[2048,768]{1,0:T(8,128)(2,1)} %bitcast.8, ...), custom_call_target="tpu_custom_call" | custom-call | tf_op jit(solution)/shard_map/moe_layer/pallas_call | solution.py:522
  174.0 1.9 %copy.10 = bf16[128,2048]{1,0:T(8,128)(2,1)} copy(bf16[128,2048]{1,0:T(8,128)(2,1)} %moe_layer.1) | data formatting | bytes 1048576

commit v8 on v7

--- a/solution.py
+++ b/solution.py
@@ -15,6 +15,7 @@
 SPLIT = 2
 AHEAD = 6
 LEAD = 2
+LAG = 3
 
 
 def dotf(a, b):
@@ -431,15 +432,17 @@
         pl.when(me != 0)(others_wait)
     with jax.named_scope("hscatter"):
         hot_scatter()
-    ahead = min(AHEAD, chunks)
-    pl.loop(0, LEAD)(send_chunk)
-    with jax.named_scope("hplane"):
-        hot_plane()
-    pl.loop(LEAD, ahead)(send_chunk)
+    pl.loop(0, 4)(send_chunk)
     with jax.named_scope("fweights"):
         pl.loop(0, chunks)(fill_weights)
     with jax.named_scope("psent0"):
-        pl.loop(0, LEAD)(pass_on_sent)
+        pass_on_sent(0)
+    pl.loop(4, min(5, chunks))(send_chunk)
+    with jax.named_scope("hplane"):
+        hot_plane()
+    with jax.named_scope("psent1"):
+        pass_on_sent(1)
+    pl.loop(min(5, chunks), min(AHEAD, chunks))(send_chunk)
 
     @pl.loop(0, chunks)
     def _(q):
@@ -456,14 +459,14 @@
 
         return_chunk(q)
 
-        @pl.when(q < chunks - ahead)
-        def _():
-            send_chunk(q + ahead)
-
-        @pl.when(q > 0)
+        @pl.when(q < chunks - AHEAD)
+        def _():
+            send_chunk(q + AHEAD)
+
+        @pl.when(q >= LAG)
         def _():
             with jax.named_scope("pret"):
-                pass_on_returned(q - 1)
+                pass_on_returned(q - LAG)
 
         @pl.when(q == 1)
         def _():
@@ -475,12 +478,15 @@
             with jax.named_scope("hopp"):
                 hot_opposite()
 
+    @pl.loop(0, LAG)
+    def _(j):
+        with jax.named_scope("pretlast"):
+            pass_on_returned(chunks - LAG + j)
+        add_returned(j)
+
     with jax.named_scope("hcore"):
         hot_core()
-    pl.loop(0, chunks // 2)(add_returned)
-    with jax.named_scope("pretlast"):
-        pass_on_returned(chunks - 1)
-    pl.loop(chunks // 2, chunks - 1)(add_returned)
+    pl.loop(LAG, chunks - 1)(add_returned)
     with jax.named_scope("hfinish"):
         hot_finish()
     add_returned(chunks - 1)

time: 176 us -> 173 us (0.983)
  the two profiles are of different devices: /device:TPU:1 before, /device:TPU:0 now
where the time goes in v8:
time: 173 us; the launch traced here: 172 us
  Pallas kernels  170 us (98%)
  local copies, waits for them, and re-layouts  1.88 us (1%)
    pallas_call x1, Pallas kernels, local_layer(): pl.pallas_call(functools.partial(layer_kernel, n), out_shape=jax.ShapeDty...  170 us

profile of v8, /device:TPU:0, one launch (start us, length us, event | category | flops | bytes accessed | tf_op | source)
XLA Modules:
  0.0 172.3 jit_solution(5436317505715741494)
XLA Ops:
  0.0 170.4 %moe_layer.1 = bf16[128,2048]{1,0:T(8,128)(2,1)} custom-call(s32[8,128]{1,0:T(8,128)} %bitcast.10, f32[8,128]{1,0:T(8,128)} %bitcast.11, s32[1,64]{1,0:T(1,128)} %bitcast.12, f32[1,64]{1,0:T(1,128)} %bitcast.13, bf16[128,2048]{1,0:T(8,128)(2,1)} %x_ref.1, bf16[2048,768]{1,0:T(8,128)(2,1)} %bitcast.7, bf16[2048,768]{1,0:T(8,128)(2,1)} %bitcast.8, ...), custom_call_target="tpu_custom_call" | custom-call | tf_op jit(solution)/shard_map/moe_layer/pallas_call | solution.py:528
  170.5 1.9 %copy.10 = bf16[128,2048]{1,0:T(8,128)(2,1)} copy(bf16[128,2048]{1,0:T(8,128)(2,1)} %moe_layer.1) | data formatting | bytes 1048576

commit v9 on v8

--- a/solution.py
+++ b/solution.py
@@ -13,8 +13,7 @@
 FOLD = 8
 VMEM_LIMIT = 60 * 1024 * 1024
 SPLIT = 2
-AHEAD = 6
-LEAD = 2
+LEAD = 4
 LAG = 3
 
 
@@ -430,19 +429,22 @@
         pl.when(me == 0)(hot_root)
     with jax.named_scope("barrier"):
         pl.when(me != 0)(others_wait)
-    with jax.named_scope("hscatter"):
-        hot_scatter()
-    pl.loop(0, 4)(send_chunk)
+    half = chunks // 2
+    pl.loop(0, half)(send_chunk)
     with jax.named_scope("fweights"):
         pl.loop(0, chunks)(fill_weights)
     with jax.named_scope("psent0"):
         pass_on_sent(0)
-    pl.loop(4, min(5, chunks))(send_chunk)
+    with jax.named_scope("hscatter"):
+        hot_scatter()
+    pl.loop(half, half + half // 2)(send_chunk)
+    with jax.named_scope("psent1"):
+        pass_on_sent(1)
+    pl.loop(half + half // 2, chunks)(send_chunk)
+    with jax.named_scope("psent23"):
+        pl.loop(2, min(LEAD, chunks))(pass_on_sent)
     with jax.named_scope("hplane"):
         hot_plane()
-    with jax.named_scope("psent1"):
-        pass_on_sent(1)
-    pl.loop(min(5, chunks), min(AHEAD, chunks))(send_chunk)
 
     @pl.loop(0, chunks)
     def _(q):
@@ -459,21 +461,17 @@
 
         return_chunk(q)
 
-        @pl.when(q < chunks - AHEAD)
-        def _():
-            send_chunk(q + AHEAD)
-
         @pl.when(q >= LAG)
         def _():
             with jax.named_scope("pret"):
                 pass_on_returned(q - LAG)
 
-        @pl.when(q == 1)
+        @pl.when(q == chunks // 2 - 1)
         def _():
             with jax.named_scope("hline"):
                 hot_line()
 
-        @pl.when(q == chunks // 2)
+        @pl.when(q == chunks - 2)
         def _():
             with jax.named_scope("hopp"):
                 hot_opposite()

time: 173 us -> 168 us (0.971)
  the two profiles are of different devices: /device:TPU:0 before, /device:TPU:2 now
where the time goes in v9:
time: 168 us; the launch traced here: 166 us
  Pallas kernels  164 us (98%)
  local copies, waits for them, and re-layouts  1.88 us (1%)
    pallas_call x1, Pallas kernels, local_layer(): pl.pallas_call(functools.partial(layer_kernel, n), out_shape=jax.ShapeDty...  164 us

profile of v9, /device:TPU:2, one launch (start us, length us, event | category | flops | bytes accessed | tf_op | source)
XLA Modules:
  0.0 166.4 jit_solution(6176484153340411494)
XLA Ops:
  0.0 164.5 %moe_layer.1 = bf16[128,2048]{1,0:T(8,128)(2,1)} custom-call(s32[8,128]{1,0:T(8,128)} %bitcast.10, f32[8,128]{1,0:T(8,128)} %bitcast.11, s32[1,64]{1,0:T(1,128)} %bitcast.12, f32[1,64]{1,0:T(1,128)} %bitcast.13, bf16[128,2048]{1,0:T(8,128)(2,1)} %x_ref.1, bf16[2048,768]{1,0:T(8,128)(2,1)} %bitcast.7, bf16[2048,768]{1,0:T(8,128)(2,1)} %bitcast.8, ...), custom_call_target="tpu_custom_call" | custom-call | tf_op jit(solution)/shard_map/moe_layer/pallas_call | solution.py:526
  164.5 1.9 %copy.10 = bf16[128,2048]{1,0:T(8,128)(2,1)} copy(bf16[128,2048]{1,0:T(8,128)(2,1)} %moe_layer.1) | data formatting | bytes 1048576

commit v10 on v9

--- a/solution.py
+++ b/solution.py
@@ -14,7 +14,7 @@
 VMEM_LIMIT = 60 * 1024 * 1024
 SPLIT = 2
 LEAD = 4
-LAG = 3
+LAG = 6
 
 
 def dotf(a, b):
@@ -461,30 +461,36 @@
 
         return_chunk(q)
 
-        @pl.when(q >= LAG)
+        @pl.when(q >= min(LAG, chunks))
         def _():
             with jax.named_scope("pret"):
-                pass_on_returned(q - LAG)
-
-        @pl.when(q == chunks // 2 - 1)
+                pass_on_returned(q - min(LAG, chunks))
+
+        @pl.when(q == 2)
         def _():
             with jax.named_scope("hline"):
                 hot_line()
 
-        @pl.when(q == chunks - 2)
+    lag = min(LAG, chunks)
+
+    @pl.loop(0, lag)
+    def _(j):
+        with jax.named_scope("pretlast"):
+            pass_on_returned(chunks - lag + j)
+
+        @pl.when(j == lag // 3)
         def _():
             with jax.named_scope("hopp"):
                 hot_opposite()
 
-    @pl.loop(0, LAG)
-    def _(j):
-        with jax.named_scope("pretlast"):
-            pass_on_returned(chunks - LAG + j)
-        add_returned(j)
-
+        @pl.when(j >= lag // 2)
+        def _():
+            add_returned(j - lag // 2)
+
+    pl.loop(lag - lag // 2, chunks // 2)(add_returned)
     with jax.named_scope("hcore"):
         hot_core()
-    pl.loop(LAG, chunks - 1)(add_returned)
+    pl.loop(chunks // 2, chunks - 1)(add_returned)
     with jax.named_scope("hfinish"):
         hot_finish()
     add_returned(chunks - 1)

time: 168 us -> 170 us (1.012)
  no operation moved by 1% of the time
where the time goes in v10:
time: 170 us; the launch traced here: 167 us
  Pallas kernels  165 us (97%)
  local copies, waits for them, and re-layouts  1.88 us (1%)
    pallas_call x1, Pallas kernels, local_layer(): pl.pallas_call(functools.partial(layer_kernel, n), out_shape=jax.ShapeDty...  165 us

profile of v10, /device:TPU:2, one launch (start us, length us, event | category | flops | bytes accessed | tf_op | source)
XLA Modules:
  0.0 167.1 jit_solution(12640694329747983698)
XLA Ops:
  0.0 165.2 %moe_layer.1 = bf16[128,2048]{1,0:T(8,128)(2,1)} custom-call(s32[8,128]{1,0:T(8,128)} %bitcast.10, f32[8,128]{1,0:T(8,128)} %bitcast.11, s32[1,64]{1,0:T(1,128)} %bitcast.12, f32[1,64]{1,0:T(1,128)} %bitcast.13, bf16[128,2048]{1,0:T(8,128)(2,1)} %x_ref.1, bf16[2048,768]{1,0:T(8,128)(2,1)} %bitcast.7, bf16[2048,768]{1,0:T(8,128)(2,1)} %bitcast.8, ...), custom_call_target="tpu_custom_call" | custom-call | tf_op jit(solution)/shard_map/moe_layer/pallas_call | solution.py:532
  165.2 1.9 %copy.10 = bf16[128,2048]{1,0:T(8,128)(2,1)} copy(bf16[128,2048]{1,0:T(8,128)(2,1)} %moe_layer.1) | data formatting | bytes 1048576

commit v11 on v10

--- a/solution.py
+++ b/solution.py
@@ -372,8 +372,7 @@
     width = 256 if d_ff % 256 == 0 else d_ff
 
     def expert(q):
-        with jax.named_scope("wrecv"):
-            wait_chunk(q, recv, recv_sem)
+        wait_chunk(q, recv, recv_sem)
         load_rows(q, recv)
         for w in range(d_ff // width):
             cols = slice(w * width, (w + 1) * width)
@@ -408,8 +407,7 @@
         weight_ref[q, :, main:] = three_terms(weights(blocks, 1).T)
 
     def add_returned(q):
-        with jax.named_scope("wback"):
-            wait_chunk(q, back, back_sem)
+        wait_chunk(q, back, back_sem)
         load_rows(q, back)
         for f in range(FOLD):
             cols = slice(f * piece, (f + 1) * piece)
@@ -421,37 +419,27 @@
             copy.wait()
         pl.semaphore_wait(barrier, devices - 1)
 
-    with jax.named_scope("fill"):
-        pl.loop(0, chunks)(fill)
+    pl.loop(0, chunks)(fill)
     recv[0, 0] = send[0, 0]
     acc_ref[...] = jnp.zeros_like(acc_ref)
-    with jax.named_scope("root"):
-        pl.when(me == 0)(hot_root)
-    with jax.named_scope("barrier"):
-        pl.when(me != 0)(others_wait)
+    pl.when(me == 0)(hot_root)
+    pl.when(me != 0)(others_wait)
     half = chunks // 2
     pl.loop(0, half)(send_chunk)
-    with jax.named_scope("fweights"):
-        pl.loop(0, chunks)(fill_weights)
-    with jax.named_scope("psent0"):
-        pass_on_sent(0)
-    with jax.named_scope("hscatter"):
-        hot_scatter()
+    pl.loop(0, chunks)(fill_weights)
+    pass_on_sent(0)
     pl.loop(half, half + half // 2)(send_chunk)
-    with jax.named_scope("psent1"):
-        pass_on_sent(1)
+    pass_on_sent(1)
+    hot_scatter()
     pl.loop(half + half // 2, chunks)(send_chunk)
-    with jax.named_scope("psent23"):
-        pl.loop(2, min(LEAD, chunks))(pass_on_sent)
-    with jax.named_scope("hplane"):
-        hot_plane()
+    pl.loop(2, min(LEAD, chunks))(pass_on_sent)
+    hot_plane()
 
     @pl.loop(0, chunks)
     def _(q):
         @pl.when(q < chunks - LEAD)
         def _():
-            with jax.named_scope("psent"):
-                pass_on_sent(q + LEAD)
+            pass_on_sent(q + LEAD)
 
         expert(q)
 
@@ -463,36 +451,30 @@
 
         @pl.when(q >= min(LAG, chunks))
         def _():
-            with jax.named_scope("pret"):
-                pass_on_returned(q - min(LAG, chunks))
-
-        @pl.when(q == 2)
-        def _():
-            with jax.named_scope("hline"):
-                hot_line()
+            pass_on_returned(q - min(LAG, chunks))
+
+        @pl.when(q == chunks // 2 + 1)
+        def _():
+            hot_line()
 
     lag = min(LAG, chunks)
 
     @pl.loop(0, lag)
     def _(j):
-        with jax.named_scope("pretlast"):
-            pass_on_returned(chunks - lag + j)
-
-        @pl.when(j == lag // 3)
-        def _():
-            with jax.named_scope("hopp"):
-                hot_opposite()
+        pass_on_returned(chunks - lag + j)
+
+        @pl.when(j == lag // 2)
+        def _():
+            hot_opposite()
 
         @pl.when(j >= lag // 2)
         def _():
             add_returned(j - lag // 2)
 
     pl.loop(lag - lag // 2, chunks // 2)(add_returned)
-    with jax.named_scope("hcore"):
-        hot_core()
+    hot_core()
     pl.loop(chunks // 2, chunks - 1)(add_returned)
-    with jax.named_scope("hfinish"):
-        hot_finish()
+    hot_finish()
     add_returned(chunks - 1)
     y_ref[...] = acc_ref[...].astype(BF16)
 
@@ -503,8 +485,7 @@
         if relayed:
             wait_relay(q, relay_out, on_sem.at[0, q])
             wait_relay(q, relay_back, on_sem.at[1, q])
-    with jax.named_scope("hsend"):
-        hot_sends_done()
+    hot_sends_done()
 
 
 def solution(mesh):

time: 170 us -> 171 us (level)
  no operation moved by 1% of the time
where the time goes in v11:
time: 171 us; the launch traced here: 168 us
  Pallas kernels  166 us (97%)
  local copies, waits for them, and re-layouts  1.88 us (1%)
    pallas_call x1, Pallas kernels, local_layer(): pl.pallas_call(functools.partial(layer_kernel, n), out_shape=jax.ShapeDty...  166 us

profile of v11, /device:TPU:2, one launch (start us, length us, event | category | flops | bytes accessed | tf_op | source)
XLA Modules:
  0.0 167.7 jit_solution(8261143366184556667)
XLA Ops:
  0.0 165.8 %moe_layer.1 = bf16[128,2048]{1,0:T(8,128)(2,1)} custom-call(s32[8,128]{1,0:T(8,128)} %bitcast.10, f32[8,128]{1,0:T(8,128)} %bitcast.11, s32[1,64]{1,0:T(1,128)} %bitcast.12, f32[1,64]{1,0:T(1,128)} %bitcast.13, bf16[128,2048]{1,0:T(8,128)(2,1)} %x_ref.1, bf16[2048,768]{1,0:T(8,128)(2,1)} %bitcast.7, bf16[2048,768]{1,0:T(8,128)(2,1)} %bitcast.8, ...), custom_call_target="tpu_custom_call" | custom-call | tf_op jit(solution)/shard_map/moe_layer/pallas_call | solution.py:513
  165.8 1.9 %copy.10 = bf16[128,2048]{1,0:T(8,128)(2,1)} copy(bf16[128,2048]{1,0:T(8,128)(2,1)} %moe_layer.1) | data formatting | bytes 1048576

commit v12 on v11

--- a/solution.py
+++ b/solution.py
@@ -72,16 +72,15 @@
         return k == n // 2
 
     def is_relayed(q, i):
-        _, kx, ky, kz = steps(q, i)
-        return jnp.logical_or(jnp.logical_or(opposite(kx), opposite(ky)), opposite(kz))
+        kc, kx, ky, kz = steps(q, i)
+        return jnp.logical_and(kc == 1, jnp.logical_or(jnp.logical_or(opposite(kx), opposite(ky)), opposite(kz)))
 
     def relay_count(q):
-        return sum(any(opposite(k) for k in steps(q, i)[1:]) for i in range(blocks))
+        return sum(any(opposite(k) for k in steps(q, i)[1:]) for i in range(1, blocks, 2))
 
     def hop(q, i, sign, leg):
         kc, kx, ky, kz = steps(q, i)
-        way = jnp.where(kc == 0, 1, n - 1)
-        move = [jnp.where(opposite(k), way, k if leg == 0 else 0) for k in (kz, ky, kx)]
+        move = [jnp.where(opposite(k), n - 1, k if leg == 0 else 0) for k in (kz, ky, kx)]
         if sign < 0:
             move = [n - m for m in move]
         return device(mz + move[0], my + move[1], mx + move[2], c + kc if leg == 0 else c)
@@ -433,7 +432,6 @@
     hot_scatter()
     pl.loop(half + half // 2, chunks)(send_chunk)
     pl.loop(2, min(LEAD, chunks))(pass_on_sent)
-    hot_plane()
 
     @pl.loop(0, chunks)
     def _(q):
@@ -446,6 +444,7 @@
         @pl.when(q == 0)
         def _():
             back[0, 0] = out[0, 0]
+            hot_plane()
 
         return_chunk(q)
 

time: 171 us -> 185 us (1.082)
  Pallas kernels: 166 us -> 181 us
    pallas_call x1, Pallas kernels: 166 us -> 181 us  [local_layer(): pl.pallas_call(functools.partial(layer_kernel, n), out_shape=jax.ShapeDty...]
where the time goes in v12:
time: 185 us; the launch traced here: 183 us
  Pallas kernels  181 us (98%)
  local copies, waits for them, and re-layouts  1.88 us (1%)
    pallas_call x1, Pallas kernels, local_layer(): pl.pallas_call(functools.partial(layer_kernel, n), out_shape=jax.ShapeDty...  181 us

profile of v12, /device:TPU:2, one launch (start us, length us, event | category | flops | bytes accessed | tf_op | source)
XLA Modules:
  0.0 183.2 jit_solution(9031348766726288280)
XLA Ops:
  0.0 181.3 %moe_layer.1 = bf16[128,2048]{1,0:T(8,128)(2,1)} custom-call(s32[8,128]{1,0:T(8,128)} %bitcast.10, f32[8,128]{1,0:T(8,128)} %bitcast.11, s32[1,64]{1,0:T(1,128)} %bitcast.12, f32[1,64]{1,0:T(1,128)} %bitcast.13, bf16[128,2048]{1,0:T(8,128)(2,1)} %x_ref.1, bf16[2048,768]{1,0:T(8,128)(2,1)} %bitcast.7, bf16[2048,768]{1,0:T(8,128)(2,1)} %bitcast.8, ...), custom_call_target="tpu_custom_call" | custom-call | tf_op jit(solution)/shard_map/moe_layer/pallas_call | solution.py:512
  181.3 1.9 %copy.10 = bf16[128,2048]{1,0:T(8,128)(2,1)} copy(bf16[128,2048]{1,0:T(8,128)(2,1)} %moe_layer.1) | data formatting | bytes 1048576

commit v13 on v11

--- a/solution.py
+++ b/solution.py
@@ -433,7 +433,6 @@
     hot_scatter()
     pl.loop(half + half // 2, chunks)(send_chunk)
     pl.loop(2, min(LEAD, chunks))(pass_on_sent)
-    hot_plane()
 
     @pl.loop(0, chunks)
     def _(q):
@@ -446,6 +445,7 @@
         @pl.when(q == 0)
         def _():
             back[0, 0] = out[0, 0]
+            hot_plane()
 
         return_chunk(q)
 

time: 171 us -> 171 us (level)
  no operation moved by 1% of the time
where the time goes in v13:
time: 171 us; the launch traced here: 168 us
  Pallas kernels  166 us (97%)
  local copies, waits for them, and re-layouts  1.88 us (1%)
    pallas_call x1, Pallas kernels, local_layer(): pl.pallas_call(functools.partial(layer_kernel, n), out_shape=jax.ShapeDty...  166 us

profile of v13, /device:TPU:2, one launch (start us, length us, event | category | flops | bytes accessed | tf_op | source)
XLA Modules:
  0.0 167.7 jit_solution(17118425290735961634)
XLA Ops:
  0.0 165.8 %moe_layer.1 = bf16[128,2048]{1,0:T(8,128)(2,1)} custom-call(s32[8,128]{1,0:T(8,128)} %bitcast.10, f32[8,128]{1,0:T(8,128)} %bitcast.11, s32[1,64]{1,0:T(1,128)} %bitcast.12, f32[1,64]{1,0:T(1,128)} %bitcast.13, bf16[128,2048]{1,0:T(8,128)(2,1)} %x_ref.1, bf16[2048,768]{1,0:T(8,128)(2,1)} %bitcast.7, bf16[2048,768]{1,0:T(8,128)(2,1)} %bitcast.8, ...), custom_call_target="tpu_custom_call" | custom-call | tf_op jit(solution)/shard_map/moe_layer/pallas_call | solution.py:513
  165.8 1.9 %copy.10 = bf16[128,2048]{1,0:T(8,128)(2,1)} copy(bf16[128,2048]{1,0:T(8,128)(2,1)} %moe_layer.1) | data formatting | bytes 1048576
